TPU v7x, 32 devices: a whole 2x2x4 slice. The times are simulated.
32 devices in a mesh: row: 4 (over y, core), col: 8 (over z, x).
Axes of the slice: x: 2, y: 2, z: 4, core: 2. Of those that a mesh axis runs over, the one named last changes fastest.
Arguments:
- amplitudes: float32 [48, 256, 1024], P('col', None, 'row'), may hold values from -6 to 6
- interaction: float32 [8192, 8192], P('row', 'col'), may hold values from -0.5 to 0.5, as said below
- tile_counts: int32 [8], replicated, may hold values from 2 to 6, as said below
- tile_block: int32 [48], replicated, may hold values from -1 to 31, as said below
- recouple_sign: int32 [48], replicated, may hold values from 0 to 1
- orbit_perm: int32 [48, 256], replicated, may hold values from 0 to 255, each once within a row
- particle_energy: float32 [48, 256], P('col'), may hold values from -2 to 2
Outputs:
- sigma: float32 [48, 256, 1024], P('col', None, 'row')
Inputs may be any that keep to these rules, and one draw needn't show every extreme that they name: Owner c holds its live tiles in its first tile_counts[c] slots; the counts sum to 32, and some owner holds 6. `tile_block`: live slots map one to one onto the 32 cross-channel tiles, and slots that are not live hold -1; two live tiles of one owner never lie in the same aligned group of 4 cross-channel tiles. interaction equals its transpose.
All inputs are finite; a program needn't handle non-finite values.
Results may differ from a plain program's by a relative error of at most 0.000061.
Values sent between devices are 32-bit elements; how exact they have to be, the bound alone decides.
No kernel may reach another device: no remote copies, remote signals or barrier semaphores. Data moves between devices by JAX's collectives and lax.ppermute only.
A program may use at most 128 MiB of HBM per device.

v0:
```python
import jax
import jax.numpy as jnp
from jax import lax
from jax.sharding import PartitionSpec as P


def tile_recouple(tiles, phases, orders):
    moved = jax.vmap(lambda single, ordering: jnp.take(single, ordering, axis=0))(tiles, orders)
    return moved * phases[:, None, None]


def local(
    amplitudes, interaction, tile_counts, tile_block, recouple_sign, orbit_perm, particle_energy
):
    column_index = lax.axis_index("col")
    row_index = lax.axis_index("row")
    column_count = lax.axis_size("col")
    slots, tile_rows, narrow_cols = amplitudes.shape
    row_blocks = interaction.shape[0] // tile_rows
    col_blocks = interaction.shape[1] // tile_rows
    tile_total = tile_block.shape[0]
    slot_ids = jnp.arange(slots, dtype=jnp.int32)
    is_live = slot_ids < jnp.take(tile_counts, column_index)
    live_mask = is_live.astype(jnp.float32)[:, None, None]
    own_block = jnp.where(
        is_live, lax.dynamic_slice_in_dim(tile_block, column_index * slots, slots), -1
    )
    all_phases = (1 - 2 * recouple_sign).astype(jnp.float32)
    own_phases = lax.dynamic_slice_in_dim(all_phases, column_index * slots, slots)
    own_orders = lax.dynamic_slice_in_dim(orbit_perm, column_index * slots, slots, 0)
    diagonal = particle_energy[:, :, None] * amplitudes
    tile_ids = jnp.arange(tile_total, dtype=jnp.int32)
    peer_ids = jnp.arange(column_count, dtype=jnp.int32)

    def tiles_of(blocks):
        matches = tile_block[None, :] == blocks[:, None]
        return jnp.sum(jnp.where(matches, tile_ids[None, :], 0), axis=1)

    target_col = own_block // col_blocks
    my_blocks = column_index * col_blocks + jnp.arange(col_blocks, dtype=jnp.int32)
    block_tiles = tiles_of(my_blocks)
    widened = lax.all_gather(amplitudes, "row", axis=2, tiled=True)
    widened = tile_recouple(widened, own_phases, own_orders)
    group_blocks = row_index * row_blocks + jnp.arange(row_blocks, dtype=jnp.int32)
    group_tiles = tiles_of(group_blocks)
    is_owned = group_tiles // slots == column_index
    placed = (
        jnp.take(widened, group_tiles % slots, axis=0) * is_owned.astype(jnp.float32)[:, None, None]
    )
    crossed = lax.psum(placed.reshape(row_blocks * tile_rows, widened.shape[2]), "col")
    partial_cols = lax.dot_general(
        interaction,
        crossed,
        (((0,), (0,)), ((), ())),
        precision=lax.Precision.HIGHEST,
        preferred_element_type=jnp.float32,
    )
    own_part = lax.psum_scatter(partial_cols, "row", scatter_dimension=1, tiled=True)
    blocks_here = own_part.reshape(col_blocks, tile_rows, narrow_cols)
    block_inverse = jnp.argsort(jnp.take(orbit_perm, block_tiles, axis=0), axis=1)
    blocks_here = tile_recouple(blocks_here, jnp.take(all_phases, block_tiles), block_inverse)
    block_owner = block_tiles // slots
    choose_mask = block_owner[None, :] == peer_ids[:, None]
    choose_block = jnp.sum(
        jnp.where(choose_mask, jnp.arange(col_blocks, dtype=jnp.int32)[None, :], 0), axis=1
    )
    choose_weight = jnp.max(choose_mask.astype(jnp.float32), axis=1)
    outgoing = jnp.take(blocks_here, choose_block, axis=0) * choose_weight[:, None, None]
    arrived = lax.all_to_all(outgoing, "col", split_axis=0, concat_axis=0, tiled=True)
    returned = jnp.take(arrived, jnp.clip(target_col, 0, column_count - 1), axis=0)
    return (returned + diagonal) * live_mask


def solution(mesh):
    placed = (P("col", None, "row"), P("row", "col"), P(), P(), P(), P(), P("col", None))
    return jax.shard_map(
        local, mesh=mesh, in_specs=placed, out_specs=P("col", None, "row"), check_vma=False
    )
```

profile of v0, /device:TPU:0, one launch (start us, length us, event | category | flops | bytes accessed | tf_op | source)
XLA Modules:
  0.0 530.1 jit_solution(5683541795034638029)
XLA Ops:
  7.4 0.7 all-gather.2.cloned.1.call-update
  8.1 0.7 subtract_convert_fusion
  8.9 0.7 bitcast_or_fusion
  9.6 0.8 select_reduce_fusion
  10.7 0.7 compare_and_fusion
  11.4 47.4 %all-gather.2.cloned.1.call-done = f32[6,256,1024]{2,1,0:T(8,128)} async-done(((f32[6,256,256]{2,1,0:T(8,128)}), f32[6,256,1024]{2,1,0:T(8,128)}) %all-gather.2.cloned.1.call-update) | async-done | bytes 6291472 | tf_op jit(solution)/shard_map/all_gather | solution.py:42
  58.8 30.4 %gather_fusion.5 = f32[1536,1024]{1,0:T(8,128)} fusion(f32[6,256,1024]{2,1,0:T(8,128)} %all-gather.2.cloned.1.call-done, s32[1536]{0:T(1024)S(1)} %reshape.217), kind=kCustom, calls=%fused_computation.5 | custom fusion | bytes 12595200 | tf_op jit(solution)/shard_map/vmap(jit(_take))/gather | solution.py:8
  89.3 4.9 select_multiply_fusion
  94.2 7.1 %gather_fusion.1 = f32[8,256,1024]{2,1,0:T(8,128)} fusion(f32[6,256,1024]{2,1,0:T(8,128)} %select_multiply_fusion, s32[1024]{0:T(1024)S(1)} %pad_clamp_fusion.2), kind=kCustom, calls=%fused_computation.1 | custom fusion | bytes 16777248 | tf_op jit(solution)/shard_map/jit(_take)/gather | solution.py:48
  101.3 5.8 %fusion = f32[2048,1024]{1,0:T(8,128)} fusion(f32[8,256,1024]{2,1,0:T(8,128)} %gather_fusion.1, f32[2048]{0:T(1024)S(1)} %bitcast.44, pred[2048]{0:T(1024)(128)(4,1)S(1)} %broadcast_in_dim.145), kind=kLoop, calls=%fused_computation.8 | loop fusion | flops 4194304 | bytes 16787456 | tf_op jit(solution)/shard_map/mul | solution.py:48
  109.2 0.7 broadcast_select_fusion
  110.7 266.6 %all-reduce.2.cloned.1.call-done = f32[2048,1024]{1,0:T(8,128)} async-done(((f32[2048,1024]{1,0:T(8,128)}), f32[2048,1024]{1,0:T(8,128)}) %all-reduce.2.cloned.1.call-update) | async-done | bytes 8388624 | tf_op jit(solution)/shard_map/psum | solution.py:50
  377.3 31.6 %convolution_bitcast_fusion = f32[1024,1024]{0,1:T(8,128)} fusion(f32[2048,1024]{1,0:T(8,128)} %all-reduce.2.cloned.1.call-done, f32[2048,1024]{1,0:T(8,128)} %param.8), kind=kOutput, calls=%fused_computation.10 | convolution fusion | flops 25769803776 | bytes 20971520 | tf_op jit(solution)/shard_map/dot_general | solution.py:51
  409.2 0.7 fusion.1
  409.9 0.7 compare_and_fusion.1
  410.6 42.2 %reduce-scatter.2.cloned.1.call-done = f32[1024,256]{0,1:T(8,128)} async-done(((f32[1024,1024]{0,1:T(8,128)}), f32[1024,256]{0,1:T(8,128)}) %reduce-scatter.2.cloned.1.call-update) | async-done | bytes 1048592 | tf_op jit(solution)/shard_map/reduce_scatter | solution.py:58
  452.8 1.6 copy.11
  454.4 7.3 %gather_fusion.6 = f32[1024,256]{1,0:T(8,128)S(1)} fusion(f32[4,256,256]{2,1,0:T(8,128)S(1)} %bitcast.40, s32[1024]{0:T(1024)S(1)} %bitcast.41), kind=kCustom, calls=%fused_computation.6 | custom fusion | bytes 2105344 | tf_op jit(solution)/shard_map/vmap(jit(_take))/gather | solution.py:8
  461.9 0.7 gather_fusion.3
  462.6 1.6 select_multiply_fusion.1
  464.3 5.5 %all-to-all-start = ((f32[8,256,256]{2,1,0:T(8,128)}), f32[8,256,256]{2,1,0:T(8,128)S(1)}, u32[]{:S(2)}, u32[]{:S(2)}) async-start(f32[8,256,256]{2,1,0:T(8,128)} %select_multiply_fusion.1), calls=%async_computation.1 | async-start | bytes 4194304 | tf_op jit(solution)/shard_map/all_to_all | solution.py:69
  471.1 46.7 %all-to-all-done = f32[8,256,256]{2,1,0:T(8,128)S(1)} async-done(((f32[8,256,256]{2,1,0:T(8,128)}), f32[8,256,256]{2,1,0:T(8,128)S(1)}, u32[]{:S(2)}, u32[]{:S(2)}) %all-to-all-start) | async-done | bytes 2097184 | tf_op jit(solution)/shard_map/all_to_all | solution.py:69
  517.8 1.8 gather_fusion.4
  519.6 3.3 add_multiply_fusion
  (45 shorter events, 4.4 us)
Async XLA Ops:
  7.4 51.5 %all-gather.2.cloned.1.call-start = ((), (), s32[]{:S(2)}) async-start(), calls=%async_computation.2 | async-start | bytes 7864320 | tf_op jit(solution)/shard_map/all_gather | solution.py:42
  8.1 369.2 %all-reduce.2.cloned.1.call-start = ((), (), s32[]{:S(2)}) async-start(), calls=%async_computation.3 | async-start | bytes 16777216 | tf_op jit(solution)/shard_map/psum | solution.py:50
  107.1 0.7 copy-start.2
  107.1 1.5 copy-start
  107.1 302.1 %sort.19.cloned.1.call-start = ((), (), s32[]{:S(2)}) async-start(), calls=%async_computation.5 | async-start | bytes 24608 | tf_op jit(solution)/shard_map/jit(argsort)/sort | solution.py:60
  110.5 342.3 %reduce-scatter.2.cloned.1.call-start = ((), (), s32[]{:S(2)}) async-start(), calls=%async_computation.4 | async-start | bytes 5242880 | tf_op jit(solution)/shard_map/reduce_scatter | solution.py:58
  461.9 7.9 %copy-start.3 = (s32[8]{0:T(128)S(1)}, s32[8]{0:T(128)}, u32[]{:S(2)}) copy-start(s32[8]{0:T(128)} %param.9) | copy-start | bytes 100
  462.6 57.0 %copy-start.1 = (f32[6,256]{1,0:T(8,128)S(1)}, f32[6,256]{1,0:T(8,128)}, u32[]{:S(2)}) copy-start(f32[6,256]{1,0:T(8,128)} %param.13) | copy-start | bytes 18436
  464.3 53.6 %all-to-all-start = ((f32[8,256,256]{2,1,0:T(8,128)}), f32[8,256,256]{2,1,0:T(8,128)S(1)}, u32[]{:S(2)}, u32[]{:S(2)}) async-start(f32[8,256,256]{2,1,0:T(8,128)} %select_multiply_fusion.1), calls=%async_computation.1 | async-start | bytes 4194304 | tf_op jit(solution)/shard_map/all_to_all | solution.py:69
Sparse Core Ops, SparseCore 0:
  9.7 49.0 all-gather.1
  107.3 270.0 all-reduce.1
  409.1 43.6 reduce-scatter.1
Sparse Core Ops, SparseCore 1:
  110.6 2.5 sort.21.cloned.1.call-done
  (1 shorter events, 0.0 us)
where the time goes:
time: 531 us; the launch traced here: 530 us
  waiting for transfers between devices  404 us (76%)
  local copies, waits for them, and re-layouts  52.2 us (10%)
  matrix products  31.6 us (6%)
  other arithmetic  21.4 us (4%)
  between operations  15.3 us (3%)
  starting transfers between devices  5.77 us (1%)
    psum x1, waiting for transfers between devices, local(): lax.psum(placed.reshape(row_blocks * tile_rows, widened.shape[2]), 'col')  267 us
    all_gather x1, waiting for transfers between devices, local(): widened = lax.all_gather(amplitudes, 'row', axis=2, tiled=True)  47.4 us
    all_to_all x1, waiting for transfers between devices, local(): lax.all_to_all(outgoing, 'col', split_axis=0, concat_axis=0, tiled=True)  46.7 us
    reduce_scatter x1, waiting for transfers between devices, local(): lax.psum_scatter(partial_cols, 'row', scatter_dimension=1, tiled=True)  42.2 us
    gather x3, local copies, waits for them, and re-layouts, tile_recouple(): jnp.take(single, ordering, axis=0)  37.7 us
    dot_general x1, matrix products, local(): lax.dot_general(interaction, crossed, (((0,), (0,)), ((), ())), precision...  31.6 us
  transfers between devices with their start and end apart: 4, of which 4 were waited for; matrix products, arithmetic and copies ran while one was open for 2% of the time, Pallas kernels for 0%

commit v1 on v0

v1 whole, which is shorter than its diff:
```python
import functools

import jax
import jax.numpy as jnp
from jax import lax
from jax.experimental import pallas as pl
from jax.experimental.pallas import tpu as pltpu
from jax.sharding import PartitionSpec as P


def xor_pairs(count, mask):
    return [(i, i ^ mask) for i in range(count)]


def halving_order(count):
    order, bit = [0], count // 2
    while bit >= 1:
        order = order + [entry ^ bit for entry in order]
        bit //= 2
    return order


def grid_of(columns):
    across = 1
    while across * across * 4 <= columns:
        across *= 2
    return columns // across, across


def exchange(tiles):
    return lax.all_to_all(tiles, "col", split_axis=0, concat_axis=0, tiled=True)


def after(value, *others):
    return lax.optimization_barrier((value, *others))[0]


class Line:
    def __init__(self, depth, across):
        self.depth, self.across = depth, across
        self.z = lax.axis_index("col") // across

    def hop(self, value, pairs):
        links = [
            (a * self.across + x, b * self.across + x) for a, b in pairs for x in range(self.across)
        ]
        return lax.ppermute(value, "col", links)

    def sources(self):
        z, depth = self.z, self.depth
        if depth != 4:
            return [z] + [(z + depth - step) % depth for step in range(1, depth)]
        low = z < 2
        return [z, z ^ 1, jnp.where(low, 2, 1), jnp.where(low, 3, 0)]

    def gather(self, own):
        z, depth = self.z, self.depth
        if depth != 4:
            out = [(own, z)]
            for step in range(1, depth):
                pairs = [(a, (a + step) % depth) for a in range(depth)]
                out.append((self.hop(own, pairs), (z + depth - step) % depth))
            return out
        inner, low = jnp.logical_or(z == 1, z == 2), z < 2
        from_pair = self.hop(own, [(0, 1), (1, 0), (2, 3), (3, 2)])
        from_middle = self.hop(own, [(1, 2), (2, 1)])
        from_far_end = self.hop(from_pair, [(1, 2), (2, 1)])
        outward_near = self.hop(from_middle, [(1, 0), (2, 3)])
        outward_far = self.hop(from_far_end, [(1, 0), (2, 3)])
        second = jnp.where(inner, from_middle, outward_near)
        third = jnp.where(inner, from_far_end, outward_far)
        return [
            (own, z),
            (from_pair, z ^ 1),
            (second, jnp.where(low, 2, 1)),
            (third, jnp.where(low, 3, 0)),
        ]


def halves(value):
    high = value.astype(jnp.bfloat16)
    return high, (value - high.astype(jnp.float32)).astype(jnp.bfloat16)


def weights_kernel(index, weight, high, low):
    del index
    rows = weight.shape[0] * weight.shape[2]
    high[0], low[0] = halves(weight[...].reshape(rows, weight.shape[3]).T)


def turned_weights(weights, index):
    groups, _, piece, height = weights.shape
    tile, count = min(512, height), index.shape[0]
    shape = jax.ShapeDtypeStruct((count, height, groups * piece), jnp.bfloat16)
    spec = pl.BlockSpec((1, tile, groups * piece), lambda k, m, index: (k, m, 0))
    return pl.pallas_call(
        weights_kernel,
        grid_spec=pltpu.PrefetchScalarGridSpec(
            num_scalar_prefetch=1,
            grid=(count, height // tile),
            in_specs=[
                pl.BlockSpec(
                    (groups, 1, piece, tile), lambda k, m, index: (0, index[k], 0, m)
                )
            ],
            out_specs=[spec, spec],
        ),
        out_shape=[shape, shape],
        cost_estimate=pl.CostEstimate(
            flops=20 * count * groups * piece * height * 100,
            bytes_accessed=8 * count * groups * piece * height,
            transcendentals=0,
        ),
        name="turned_weights",
    )(index, weights)


def product_kernel(count, has_start, splits, *refs):
    high, low, panels = refs[:count], refs[count : 2 * count], refs[2 * count : 3 * count]
    rest = refs[3 * count :]
    outs = rest[1:] if has_start else rest
    total = rest[0][...] if has_start else None

    def dot(a, b):
        return jnp.dot(a, b, preferred_element_type=jnp.float32)

    for w_high, w_low, panel in zip(high, low, panels):
        p_high, p_low = halves(panel[...])
        more = dot(w_high[0], p_high) + (dot(w_high[0], p_low) + dot(w_low[0], p_high))
        total = more if total is None else total + more
    width = total.shape[1] // splits
    for n, out in enumerate(outs):
        out[...] = total[:, n * width : (n + 1) * width]


def summed_products(turned, first, panels, start, splits):
    count = len(panels)
    _, height, depth = turned[0].shape
    width = panels[0].shape[1]
    tile = min(512, height)

    def weight_spec(n):
        return pl.BlockSpec((1, tile, depth), lambda m: (first + n, m, 0))

    in_specs = [weight_spec(n) for n in range(count)] * 2
    in_specs += [pl.BlockSpec((depth, width), lambda m: (0, 0))] * count
    operands = [turned[0]] * count + [turned[1]] * count + list(panels)
    if start is not None:
        in_specs.append(pl.BlockSpec((tile, width), lambda m: (m, 0)))
        operands.append(start)
    shape = jax.ShapeDtypeStruct((height, width // splits), jnp.float32)
    spec = pl.BlockSpec((tile, width // splits), lambda m: (m, 0))
    return pl.pallas_call(
        functools.partial(product_kernel, count, start is not None, splits),
        grid=(height // tile,),
        in_specs=in_specs,
        out_specs=[spec] * splits,
        out_shape=[shape] * splits,
        cost_estimate=pl.CostEstimate(
            flops=6 * count * depth * height * width,
            bytes_accessed=4 * (count * depth * (height + width) + 2 * height * width),
            transcendentals=0,
        ),
        name="summed_products",
    )(*operands)


def local(
    amplitudes, interaction, tile_counts, tile_block, recouple_sign, orbit_perm, particle_energy
):
    column = lax.axis_index("col")
    row = lax.axis_index("row")
    columns = lax.axis_size("col")
    rows = lax.axis_size("row")
    depth, across = grid_of(columns)
    slots, tile_rows, narrow = amplitudes.shape
    row_blocks = interaction.shape[0] // tile_rows
    col_blocks = interaction.shape[1] // tile_rows
    tile_total = tile_block.shape[0]
    piece = tile_rows // columns
    order = halving_order(rows)

    slot_ids = jnp.arange(slots, dtype=jnp.int32)
    is_live = slot_ids < jnp.take(tile_counts, column, mode="clip")
    own_block = lax.dynamic_slice_in_dim(tile_block, column * slots, slots)
    own_phase = 1 - 2 * lax.dynamic_slice_in_dim(recouple_sign, column * slots, slots)
    own_perm = lax.dynamic_slice_in_dim(orbit_perm, column * slots, slots, 0)
    tile_ids = jnp.arange(tile_total, dtype=jnp.int32)

    def tiles_of(blocks):
        matches = tile_block[None, :] == blocks[:, None]
        return jnp.sum(jnp.where(matches, tile_ids[None, :], 0), axis=1)

    orbitals = jnp.arange(tile_rows, dtype=jnp.int32)
    recouple = jnp.where(
        own_perm[:, :, None] == orbitals[None, None, :], own_phase[:, None, None], 0
    ).astype(jnp.float32)

    weights = interaction.reshape(row_blocks, columns, piece, interaction.shape[1])
    x = column % across
    picks = {}
    for mask in order:
        blocks = (row ^ mask) * row_blocks + jnp.arange(row_blocks, dtype=jnp.int32)
        picks[mask] = tiles_of(blocks)
    my_blocks = column * col_blocks + jnp.arange(col_blocks, dtype=jnp.int32)
    owners = tiles_of(my_blocks) // slots
    peers = jnp.arange(columns, dtype=jnp.int32)
    choice = jnp.sum(
        jnp.where(
            owners[None, :] == peers[:, None], jnp.arange(col_blocks, dtype=jnp.int32)[None, :], 0
        ),
        axis=1,
    )
    source = jnp.clip(own_block // col_blocks, 0, columns - 1)
    line = Line(depth, across)

    cut = jnp.einsum("sjp,spn->sjn", recouple, amplitudes, precision=lax.Precision.HIGHEST)
    cut = cut.reshape(slots, columns, piece, narrow).transpose(1, 0, 2, 3)
    cut = exchange(cut).reshape(tile_total, piece, narrow)

    def regroup(cut):
        parts = []
        for mask in order:
            part = jnp.take(cut, picks[mask], axis=0, mode="clip")
            if mask:
                part = lax.ppermute(part, "row", xor_pairs(rows, mask))
            parts.append(part.reshape(row_blocks * piece, cut.shape[2]))
        return jnp.concatenate(parts, axis=1)

    def across_x(held, mask):
        links = [
            (a * across + b, a * across + (b ^ mask)) for a in range(depth) for b in range(across)
        ]
        return lax.ppermute(held, "col", links)

    def crossed(held):
        return [
            [(value if mask == 0 else across_x(value, mask), z, mask) for mask in range(across)]
            for value, z in held
        ]

    ways = [(n, 0) for n in range(depth)] + [(n, m) for n in range(depth) for m in range(1, across)]
    ways.sort(key=lambda way: (way[0] + 2 * way[1], way[1]) if way[1] else (way[0] + 1, 0))
    index = jnp.stack([line.sources()[n] * across + (x ^ mask) for n, mask in ways])
    turned = turned_weights(weights, index)

    def product(panels):
        values = [panels[n][mask][0] for n, mask in ways]
        total, first = None, 0
        early = len(values) - max(1, len(values) // 4)
        for name, size in (("a", early), ("c", len(values) - early)):
            last = name == "c"
            out = summed_products(
                turned, first, values[first : first + size], total, 2 if last else 1,
            )
            total, first = out[0], first + size
        return out

    def to_row(value, bit):
        return lax.ppermute(value, "row", xor_pairs(rows, bit))

    def returned(home, tiles):
        picked = jnp.take(home, source, axis=0, mode="clip")
        back = jnp.einsum("sjp,sjn->spn", recouple, picked, precision=lax.Precision.HIGHEST)
        sigma = back + particle_energy[:, :, None] * tiles
        return jnp.where(is_live[:, None, None], sigma, 0.0)

    def halved(kept, arrived):
        width = kept.shape[1] // 2
        return kept[:, :width] + arrived[:, :width], kept[:, width:] + arrived[:, width:]

    chunks = max(1, narrow // 128)
    step = narrow // chunks
    tiles = [amplitudes[:, :, k * step : (k + 1) * step] for k in range(chunks)]
    outs = []
    panels, homes = [None] * chunks, [None] * chunks
    for k in range(chunks):
        shard = regroup(cut[:, :, k * step : (k + 1) * step])
        panels[k] = crossed(line.gather(shard))
    for k in range(chunks):
        kept, sent = product(panels[k])
        bit = 1
        while True:
            arrived = to_row(sent, bit)
            bit *= 2
            if bit >= rows:
                break
            kept, sent = halved(kept, arrived)
        if k:
            arrived = after(arrived, own)
        own = kept + arrived
        here = own.reshape(col_blocks, tile_rows, own.shape[1])

        homes[k] = exchange(jnp.take(here, choice, axis=0, mode="clip"))
        if k:
            outs.append(returned(after(homes[k - 1], sent), tiles[k - 1]))
    outs.append(returned(homes[-1], tiles[-1]))
    return jnp.concatenate(outs, axis=2)


def solution(mesh):
    placed = (P("col", None, "row"), P("row", "col"), P(), P(), P(), P(), P("col", None))

    return jax.shard_map(
        local, mesh=mesh, in_specs=placed, out_specs=P("col", None, "row"), check_vma=False
    )
```

time: 531 us -> 274 us (0.52)
  waiting for transfers between devices: 404 us -> 130 us
  starting transfers between devices: 5.77 us -> 59.9 us
  Pallas kernels: 0 us -> 42.2 us
  local copies, waits for them, and re-layouts: 52.2 us -> 20.4 us
  matrix products: 31.6 us -> 7.88 us
  between operations: 15.3 us -> 0.59 us
  other arithmetic: 21.4 us -> 11.1 us
    psum x1 -> x0, waiting for transfers between devices: 267 us -> none  [local(): lax.psum(placed.reshape(row_blocks * tile_rows, widened.shape[2]), 'col')]
    ppermute x0 -> x28, waiting for transfers between devices: none -> 67.1 us  [the longest x10 26.9 us: hop(): return lax.ppermute(value, 'col', links)]
    all_gather x1 -> x0, waiting for transfers between devices: 47.4 us -> none  [local(): widened = lax.all_gather(amplitudes, 'row', axis=2, tiled=True)]
    pallas_call x0 -> x5, Pallas kernels: none -> 42.2 us  [the longest x4 28.3 us: summed_products(): pl.pallas_call(functools.partial(product_kernel, count, start is not None...]
    reduce_scatter x1 -> x0, waiting for transfers between devices: 42.2 us -> none  [local(): lax.psum_scatter(partial_cols, 'row', scatter_dimension=1, tiled=True)]
    ppermute x0 -> x28, starting transfers between devices: none -> 40.4 us  [the longest x10 24.3 us: hop(): return lax.ppermute(value, 'col', links)]
    gather x8 -> x12, local copies, waits for them, and re-layouts: 48.5 us -> 10 us  [the longest x8 4.46 us: regroup(): part = jnp.take(cut, picks[mask], axis=0, mode='clip')]
    dot_general x1 -> x3, matrix products: 31.6 us -> 7.88 us  [the longest x2 4.71 us: returned(): jnp.einsum('sjp,sjn->spn', recouple, picked, precision=lax.Precision.HIGH...]
  transfers between devices with their start and end apart: 4 -> 31, of which waited for: 4 -> 14; matrix products, arithmetic and copies ran while one was open for 2% -> 9% of each run, Pallas kernels for 0% -> 16%
where the time goes in v1:
time: 274 us; the launch traced here: 272 us
  waiting for transfers between devices  130 us (47%)
  starting transfers between devices  59.9 us (22%)
  Pallas kernels  42.2 us (15%)
  local copies, waits for them, and re-layouts  20.4 us (7%)
  other arithmetic  11.1 us (4%)
  matrix products  7.88 us (3%)
    all_to_all x3, waiting for transfers between devices, exchange(): return lax.all_to_all(tiles, 'col', split_axis=0, concat_axis=0, tiled=True)  63.1 us
    pallas_call x4, Pallas kernels, summed_products(): pl.pallas_call(functools.partial(product_kernel, count, start is not None...  28.3 us
    ppermute x10, waiting for transfers between devices, hop(): return lax.ppermute(value, 'col', links)  26.9 us
    ppermute x10, starting transfers between devices, hop(): return lax.ppermute(value, 'col', links)  24.3 us
    ppermute x8, waiting for transfers between devices, across_x(): return lax.ppermute(held, 'col', links)  21.4 us
    all_to_all x3, starting transfers between devices, exchange(): return lax.all_to_all(tiles, 'col', split_axis=0, concat_axis=0, tiled=True)  19.5 us
    pallas_call x1, Pallas kernels, turned_weights(): pl.pallas_call(weights_kernel, grid_spec=pltpu.PrefetchScalarGridSpec(num...  14 us
    ppermute x4, waiting for transfers between devices, to_row(): return lax.ppermute(value, 'row', xor_pairs(rows, bit))  12.9 us
  transfers between devices with their start and end apart: 31, of which 14 were waited for; matrix products, arithmetic and copies ran while one was open for 9% of the time, Pallas kernels for 16%

profile of v1, /device:TPU:0, one launch (start us, length us, event | category | flops | bytes accessed | tf_op | source)
XLA Modules:
  0.0 272.4 jit_solution(13046119223986493988)
XLA Ops:
  1.5 3.2 %fusion.4 = f32[6,256,256]{2,1,0:T(8,128)S(1)} fusion(f32[6,256,256]{2,1,0:T(8,128)} %param.7, s32[6]{0:T(128)S(1)} %multiply_subtract_fusion, s32[6,256]{1,0:T(8,128)S(1)} %constant_dynamic-slice_fusion), kind=kOutput, calls=%fused_computation.18 | convolution fusion | flops 1209139200 | bytes 3151896 | tf_op jit(solution)/shard_map/sjp,spn->sjn/dot_general | solution.py:217
  6.0 7.4 %all-to-all-start = ((f32[8,6,32,256]{3,2,1,0:T(8,128)}), f32[8,6,32,256]{3,2,1,0:T(8,128)S(1)}, u32[]{:S(2)}, u32[]{:S(2)}) async-start(f32[8,6,32,256]{3,2,1,0:T(8,128)} %bitcast.27), calls=%async_computation | async-start | bytes 3145728 | tf_op jit(solution)/shard_map/all_to_all | solution.py:31
  13.7 36.7 %all-to-all-done = f32[8,6,32,256]{3,2,1,0:T(8,128)S(1)} async-done(((f32[8,6,32,256]{3,2,1,0:T(8,128)}), f32[8,6,32,256]{3,2,1,0:T(8,128)S(1)}, u32[]{:S(2)}, u32[]{:S(2)}) %all-to-all-start) | async-done | bytes 1572896 | tf_op jit(solution)/shard_map/all_to_all | solution.py:31
  56.2 2.9 %collective-permute-done.2 = f32[8,32,128]{2,1,0:T(8,128)S(1)} collective-permute-done((f32[8,32,128]{2,1,0:T(8,128)S(1)}, f32[8,32,128]{2,1,0:T(8,128)S(1)}, u32[]{:S(2)}, u32[]{:S(2)}) %collective-permute-start.2) | collective-permute-done | bytes 131104 | tf_op jit(solution)/shard_map/ppermute | solution.py:226
  60.0 13.6 %collective-permute-done.6.refs_13_ = f32[256,512]{1,0:T(8,128)S(1)} collective-permute-done((f32[256,512]{1,0:T(8,128)S(1)}, f32[256,512]{1,0:T(8,128)S(1)}, u32[]{:S(2)}, u32[]{:S(2)}) %collective-permute-start.6) | collective-permute-done | bytes 524320 | tf_op jit(solution)/shard_map/ppermute | solution.py:47
  86.5 14.7 %collective-permute-start.20 = (f32[256,512]{1,0:T(8,128)S(1)}, f32[256,512]{1,0:T(8,128)S(1)}, u32[]{:S(2)}, u32[]{:S(2)}) collective-permute-start(f32[256,512]{1,0:T(8,128)S(1)} %pad_maximum_fusion.2.refs_12_), channel_id=1, source_target_pairs={{0,2},{1,3},{2,0},{3,1},{4,6},{5,7},{6,4},{7,5},{8,10},{9,11},{10,... | collective-permute-start | bytes 1572872 | tf_op jit(solution)/shard_map/ppermute | solution.py:47
  109.2 14.0 %turned_weights.1 = (bf16[8,1024,256]{2,1,0:T(8,128)(2,1)}, bf16[8,1024,256]{2,1,0:T(8,128)(2,1)}) custom-call(s32[8]{0:T(128)} %stack.35.index, f32[8,8,32,1024]{3,2,1,0:T(8,128)} %bitcast.37), custom_call_target="tpu_custom_call" | custom-call | flops 4194304000 | bytes 16777216 | tf_op jit(solution)/shard_map/turned_weights/pallas_call | solution.py:96
  126.0 9.1 %summed_products.4.refs_6_ = f32[1024,512]{1,0:T(8,128)} custom-call(bf16[8,1024,256]{2,1,0:T(8,128)(2,1)} %get-tuple-element.13.refs_0_.refs_1_.refs_2_.refs_3_.refs_4_.refs_5_, bf16[8,1024,256]{2,1,0:T(8,128)(2,1)} %get-tuple-element.13.refs_0_.refs_1_.refs_2_.refs_3_.refs_4_.refs_5_, ...), custom_call_target="tpu_custom_call" | custom-call | flops 4831838208 | bytes 13631488 | tf_op jit(solution)/shard_map/summed_products/pallas_call | solution.py:153
  135.1 4.1 %collective-permute-done.9.refs_5_ = f32[256,512]{1,0:T(8,128)S(1)} collective-permute-done((f32[256,512]{1,0:T(8,128)S(1)}, f32[256,512]{1,0:T(8,128)S(1)}, u32[]{:S(2)}, u32[]{:S(2)}) %collective-permute-start.9) | collective-permute-done | bytes 524320 | tf_op jit(solution)/shard_map/ppermute | solution.py:234
  139.9 5.1 %summed_products.5 = (f32[1024,256]{1,0:T(8,128)}, f32[1024,256]{1,0:T(8,128)}) custom-call(bf16[8,1024,256]{2,1,0:T(8,128)(2,1)} %get-tuple-element.13.refs_0_.refs_1_.refs_2_.refs_3_.refs_4_.refs_5_, bf16[8,1024,256]{2,1,0:T(8,128)(2,1)} %get-tuple-element.13.refs_0_.refs_1_.refs_2_.refs_3_.refs_4_.refs_5_, ...), custom_call_target="tpu_custom_call" | custom-call | flops 1610612736 | bytes 7340032 | tf_op jit(solution)/shard_map/summed_products/pallas_call | solution.py:153
  151.4 13.2 %collective-permute-done.22 = f32[256,512]{1,0:T(8,128)S(1)} collective-permute-done((f32[256,512]{1,0:T(8,128)}, f32[256,512]{1,0:T(8,128)S(1)}, u32[]{:S(2)}, u32[]{:S(2)}) %collective-permute-start.22) | collective-permute-done | bytes 524320 | tf_op jit(solution)/shard_map/ppermute | solution.py:47
  168.5 4.4 %collective-permute-done.25.refs_16_ = f32[256,512]{1,0:T(8,128)} collective-permute-done((f32[256,512]{1,0:T(8,128)S(1)}, f32[256,512]{1,0:T(8,128)}, u32[]{:S(2)}, u32[]{:S(2)}) %collective-permute-start.25) | collective-permute-done | bytes 524320 | tf_op jit(solution)/shard_map/ppermute | solution.py:234
  172.9 9.0 %summed_products.6.refs_6_ = f32[1024,512]{1,0:T(8,128)} custom-call(bf16[8,1024,256]{2,1,0:T(8,128)(2,1)} %get-tuple-element.13.refs_0_.refs_1_.refs_2_.refs_3_.refs_4_.refs_5_, bf16[8,1024,256]{2,1,0:T(8,128)(2,1)} %get-tuple-element.13.refs_0_.refs_1_.refs_2_.refs_3_.refs_4_.refs_5_, ...), custom_call_target="tpu_custom_call" | custom-call | flops 4831838208 | bytes 13631488 | tf_op jit(solution)/shard_map/summed_products/pallas_call | solution.py:153
  181.9 2.2 collective-permute-done.19.refs_4_
  184.1 10.8 %collective-permute-done.23.refs_5_ = f32[256,512]{1,0:T(8,128)} collective-permute-done((f32[256,512]{1,0:T(8,128)S(1)}, f32[256,512]{1,0:T(8,128)}, u32[]{:S(2)}, u32[]{:S(2)}) %collective-permute-start.23) | collective-permute-done | bytes 524320 | tf_op jit(solution)/shard_map/ppermute | solution.py:234
  194.9 5.1 %summed_products.7 = (f32[1024,256]{1,0:T(8,128)}, f32[1024,256]{1,0:T(8,128)}) custom-call(bf16[8,1024,256]{2,1,0:T(8,128)(2,1)} %get-tuple-element.13.refs_0_.refs_1_.refs_2_.refs_3_.refs_4_.refs_5_, bf16[8,1024,256]{2,1,0:T(8,128)(2,1)} %get-tuple-element.13.refs_0_.refs_1_.refs_2_.refs_3_.refs_4_.refs_5_, ...), custom_call_target="tpu_custom_call" | custom-call | flops 1610612736 | bytes 7340032 | tf_op jit(solution)/shard_map/summed_products/pallas_call | solution.py:153
  202.9 7.6 %all-to-all-start.1 = ((f32[8,256,128]{2,1,0:T(8,128)}), f32[8,256,128]{2,1,0:T(8,128)S(1)}, u32[]{:S(2)}, u32[]{:S(2)}) async-start(f32[8,256,128]{2,1,0:T(8,128)} %gather_fusion.4), calls=%async_computation.1 | async-start | bytes 2097152 | tf_op jit(solution)/shard_map/all_to_all | solution.py:31
  212.8 12.9 %collective-permute-done.27 = f32[1024,128]{1,0:T(8,128)S(1)} collective-permute-done((f32[1024,128]{1,0:T(8,128)S(1)}, f32[1024,128]{1,0:T(8,128)S(1)}, u32[]{:S(2)}, u32[]{:S(2)}) %collective-permute-start.27) | collective-permute-done | bytes 524320 | tf_op jit(solution)/shard_map/ppermute | solution.py:260
  228.4 8.5 %all-to-all-done.1 = f32[8,256,128]{2,1,0:T(8,128)S(1)} async-done(((f32[8,256,128]{2,1,0:T(8,128)}), f32[8,256,128]{2,1,0:T(8,128)S(1)}, u32[]{:S(2)}, u32[]{:S(2)}) %all-to-all-start.1) | async-done | bytes 1048608 | tf_op jit(solution)/shard_map/all_to_all | solution.py:31
  236.9 4.4 %all-to-all-start.2 = ((f32[8,256,128]{2,1,0:T(8,128)}), f32[8,256,128]{2,1,0:T(8,128)}, u32[]{:S(2)}, u32[]{:S(2)}) async-start(f32[8,256,128]{2,1,0:T(8,128)} %gather_fusion.10), calls=%async_computation.2 | async-start | bytes 2097152 | tf_op jit(solution)/shard_map/all_to_all | solution.py:31
  246.2 2.6 fusion.12
  248.8 17.9 %all-to-all-done.2 = f32[8,256,128]{2,1,0:T(8,128)} async-done(((f32[8,256,128]{2,1,0:T(8,128)}), f32[8,256,128]{2,1,0:T(8,128)}, u32[]{:S(2)}, u32[]{:S(2)}) %all-to-all-start.2) | async-done | bytes 1048608 | tf_op jit(solution)/shard_map/all_to_all | solution.py:31
  266.7 1.8 gather_fusion.11
  268.6 2.1 fusion.18
  (138 shorter events, 58.4 us)
Async XLA Ops:
  6.0 44.4 %all-to-all-start = ((f32[8,6,32,256]{3,2,1,0:T(8,128)}), f32[8,6,32,256]{3,2,1,0:T(8,128)S(1)}, u32[]{:S(2)}, u32[]{:S(2)}) async-start(f32[8,6,32,256]{3,2,1,0:T(8,128)} %bitcast.27), calls=%async_computation | async-start | bytes 3145728 | tf_op jit(solution)/shard_map/all_to_all | solution.py:31
  59.2 14.4 %collective-permute-start.6 = (f32[256,512]{1,0:T(8,128)S(1)}, f32[256,512]{1,0:T(8,128)S(1)}, u32[]{:S(2)}, u32[]{:S(2)}) collective-permute-start(f32[256,512]{1,0:T(8,128)S(1)} %pad_maximum_fusion.1.refs_12_), channel_id=1, source_target_pairs={{0,2},{1,3},{2,0},{3,1},{4,6},{5,7},{6,4},{7,5},{8,10},{9,11},{10,... | collective-permute-start | bytes 1572872 | tf_op jit(solution)/shard_map/ppermute | solution.py:47
  59.3 15.0 %collective-permute-start.3 = (f32[256,512]{1,0:T(8,128)S(1)}, f32[256,512]{1,0:T(8,128)S(1)}, u32[]{:S(2)}, u32[]{:S(2)}) collective-permute-start(f32[256,512]{1,0:T(8,128)S(1)} %pad_maximum_fusion.1.refs_12_), channel_id=1, source_target_pairs={{2,4},{3,5},{4,2},{5,3},{10,12},{11,13},{12,10},{13,11},{18,20},{1... | collective-permute-start | bytes 1572872 | tf_op jit(solution)/shard_map/ppermute | solution.py:47
  74.3 28.4 %collective-permute-start.4 = (f32[256,512]{1,0:T(8,128)S(1)}, f32[256,512]{1,0:T(8,128)}, u32[]{:S(2)}, u32[]{:S(2)}) collective-permute-start(f32[256,512]{1,0:T(8,128)S(1)} %collective-permute-done.3), channel_id=1, source_target_pairs={{2,0},{3,1},{4,6},{5,7},{10,8},{11,9},{12,14},{13,15},{18,16},{19,... | collective-permute-start | bytes 1572872 | tf_op jit(solution)/shard_map/ppermute | solution.py:47
  75.6 29.5 %collective-permute-start.8 = (f32[256,512]{1,0:T(8,128)S(1)}, f32[256,512]{1,0:T(8,128)}, u32[]{:S(2)}, u32[]{:S(2)}) collective-permute-start(f32[256,512]{1,0:T(8,128)S(1)} %collective-permute-done.7), channel_id=1, source_target_pairs={{2,0},{3,1},{4,6},{5,7},{10,8},{11,9},{12,14},{13,15},{18,16},{19,... | collective-permute-start | bytes 1572872 | tf_op jit(solution)/shard_map/ppermute | solution.py:47
  83.9 23.2 %collective-permute-start.10 = (f32[256,512]{1,0:T(8,128)S(1)}, f32[256,512]{1,0:T(8,128)S(1)}, u32[]{:S(2)}, u32[]{:S(2)}) collective-permute-start(f32[256,512]{1,0:T(8,128)S(1)} %pad_maximum_fusion.1.refs_12_), channel_id=1, source_target_pairs={{0,1},{1,0},{2,3},{3,2},{4,5},{5,4},{6,7},{7,6},{8,9},{9,8},{10,11... | collective-permute-start | bytes 1572872 | tf_op jit(solution)/shard_map/ppermute | solution.py:234
  86.5 36.7 %collective-permute-start.20 = (f32[256,512]{1,0:T(8,128)S(1)}, f32[256,512]{1,0:T(8,128)S(1)}, u32[]{:S(2)}, u32[]{:S(2)}) collective-permute-start(f32[256,512]{1,0:T(8,128)S(1)} %pad_maximum_fusion.2.refs_12_), channel_id=1, source_target_pairs={{0,2},{1,3},{2,0},{3,1},{4,6},{5,7},{6,4},{7,5},{8,10},{9,11},{10,... | collective-permute-start | bytes 1572872 | tf_op jit(solution)/shard_map/ppermute | solution.py:47
  101.2 23.5 %collective-permute-start.17 = (f32[256,512]{1,0:T(8,128)S(1)}, f32[256,512]{1,0:T(8,128)}, u32[]{:S(2)}, u32[]{:S(2)}) collective-permute-start(f32[256,512]{1,0:T(8,128)S(1)} %pad_maximum_fusion.2.refs_12_), channel_id=1, source_target_pairs={{2,4},{3,5},{4,2},{5,3},{10,12},{11,13},{12,10},{13,11},{18,20},{1... | collective-permute-start | bytes 1572872 | tf_op jit(solution)/shard_map/ppermute | solution.py:47
  102.7 23.3 %collective-permute-start.11 = (f32[256,512]{1,0:T(8,128)S(1)}, f32[256,512]{1,0:T(8,128)}, u32[]{:S(2)}, u32[]{:S(2)}) collective-permute-start(f32[256,512]{1,0:T(8,128)S(1)} %collective-permute-done.6.refs_13_), channel_id=1, source_target_pairs={{0,1},{1,0},{2,3},{3,2},{4,5},{5,4},{6,7},{7,6},{8,9},{9,8},{10,11... | collective-permute-start | bytes 1572872 | tf_op jit(solution)/shard_map/ppermute | solution.py:234
  105.1 29.9 %collective-permute-start.5 = (f32[256,512]{1,0:T(8,128)S(1)}, f32[256,512]{1,0:T(8,128)}, u32[]{:S(2)}, u32[]{:S(2)}) collective-permute-start(f32[256,512]{1,0:T(8,128)S(1)} %broadcast_select_fusion.3.refs_15_), channel_id=1, source_target_pairs={{0,1},{1,0},{2,3},{3,2},{4,5},{5,4},{6,7},{7,6},{8,9},{9,8},{10,11... | collective-permute-start | bytes 1572872 | tf_op jit(solution)/shard_map/ppermute | solution.py:234
  107.9 31.2 %collective-permute-start.9 = (f32[256,512]{1,0:T(8,128)S(1)}, f32[256,512]{1,0:T(8,128)S(1)}, u32[]{:S(2)}, u32[]{:S(2)}) collective-permute-start(f32[256,512]{1,0:T(8,128)S(1)} %broadcast_select_fusion.2.refs_17_), channel_id=1, source_target_pairs={{0,1},{1,0},{2,3},{3,2},{4,5},{5,4},{6,7},{7,6},{8,9},{9,8},{10,11... | collective-permute-start | bytes 1572872 | tf_op jit(solution)/shard_map/ppermute | solution.py:234
  123.2 22.0 %collective-permute-start.21 = (f32[256,512]{1,0:T(8,128)S(1)}, f32[256,512]{1,0:T(8,128)}, u32[]{:S(2)}, u32[]{:S(2)}) collective-permute-start(f32[256,512]{1,0:T(8,128)S(1)} %collective-permute-done.20.refs_13_), channel_id=1, source_target_pairs={{2,4},{3,5},{4,2},{5,3},{10,12},{11,13},{12,10},{13,11},{18,20},{1... | collective-permute-start | bytes 1572872 | tf_op jit(solution)/shard_map/ppermute | solution.py:47
  124.7 24.1 %collective-permute-start.18 = (f32[256,512]{1,0:T(8,128)}, f32[256,512]{1,0:T(8,128)}, u32[]{:S(2)}, u32[]{:S(2)}) collective-permute-start(f32[256,512]{1,0:T(8,128)} %collective-permute-done.17), channel_id=1, source_target_pairs={{2,0},{3,1},{4,6},{5,7},{10,8},{11,9},{12,14},{13,15},{18,16},{19,... | collective-permute-start | bytes 1572872 | tf_op jit(solution)/shard_map/ppermute | solution.py:47
  145.0 21.2 %collective-permute-start.12 = (f32[1024,256]{1,0:T(8,128)}, f32[1024,256]{1,0:T(8,128)S(1)}, u32[]{:S(2)}, u32[]{:S(2)}) collective-permute-start(f32[1024,256]{1,0:T(8,128)} %get-tuple-element.16), channel_id=1, source_target_pairs={{0,8},{8,0},{16,24},{24,16},{1,9},{9,1},{17,25},{25,17},{2,10},{10... | collective-permute-start | bytes 3145736 | tf_op jit(solution)/shard_map/ppermute | solution.py:260
  145.2 19.4 %collective-permute-start.22 = (f32[256,512]{1,0:T(8,128)}, f32[256,512]{1,0:T(8,128)S(1)}, u32[]{:S(2)}, u32[]{:S(2)}) collective-permute-start(f32[256,512]{1,0:T(8,128)} %collective-permute-done.21), channel_id=1, source_target_pairs={{2,0},{3,1},{4,6},{5,7},{10,8},{11,9},{12,14},{13,15},{18,16},{19,... | collective-permute-start | bytes 1572872 | tf_op jit(solution)/shard_map/ppermute | solution.py:47
  146.6 21.0 %collective-permute-start.24 = (f32[256,512]{1,0:T(8,128)S(1)}, f32[256,512]{1,0:T(8,128)S(1)}, u32[]{:S(2)}, u32[]{:S(2)}) collective-permute-start(f32[256,512]{1,0:T(8,128)S(1)} %pad_maximum_fusion.2.refs_12_), channel_id=1, source_target_pairs={{0,1},{1,0},{2,3},{3,2},{4,5},{5,4},{6,7},{7,6},{8,9},{9,8},{10,11... | collective-permute-start | bytes 1572872 | tf_op jit(solution)/shard_map/ppermute | solution.py:234
  148.1 24.7 %collective-permute-start.25 = (f32[256,512]{1,0:T(8,128)S(1)}, f32[256,512]{1,0:T(8,128)}, u32[]{:S(2)}, u32[]{:S(2)}) collective-permute-start(f32[256,512]{1,0:T(8,128)S(1)} %collective-permute-done.20.refs_13_), channel_id=1, source_target_pairs={{0,1},{1,0},{2,3},{3,2},{4,5},{5,4},{6,7},{7,6},{8,9},{9,8},{10,11... | collective-permute-start | bytes 1572872 | tf_op jit(solution)/shard_map/ppermute | solution.py:234
  149.9 34.2 %collective-permute-start.19 = (f32[256,512]{1,0:T(8,128)S(1)}, f32[256,512]{1,0:T(8,128)}, u32[]{:S(2)}, u32[]{:S(2)}) collective-permute-start(f32[256,512]{1,0:T(8,128)S(1)} %broadcast_select_fusion.1.refs_15_), channel_id=1, source_target_pairs={{0,1},{1,0},{2,3},{3,2},{4,5},{5,4},{6,7},{7,6},{8,9},{9,8},{10,11... | collective-permute-start | bytes 1572872 | tf_op jit(solution)/shard_map/ppermute | solution.py:234
  164.7 30.1 %collective-permute-start.23 = (f32[256,512]{1,0:T(8,128)S(1)}, f32[256,512]{1,0:T(8,128)}, u32[]{:S(2)}, u32[]{:S(2)}) collective-permute-start(f32[256,512]{1,0:T(8,128)S(1)} %broadcast_select_fusion.refs_17_), channel_id=1, source_target_pairs={{0,1},{1,0},{2,3},{3,2},{4,5},{5,4},{6,7},{7,6},{8,9},{9,8},{10,11... | collective-permute-start | bytes 1572872 | tf_op jit(solution)/shard_map/ppermute | solution.py:234
  167.2 32.8 %collective-permute-start.13 = (f32[1024,128]{1,0:T(8,128)}, f32[1024,128]{1,0:T(8,128)}, u32[]{:S(2)}, u32[]{:S(2)}) collective-permute-start(f32[1024,128]{1,0:T(8,128)} %slice_add_fusion.2), channel_id=1, source_target_pairs={{0,16},{8,24},{16,0},{24,8},{1,17},{9,25},{17,1},{25,9},{2,18},{10... | collective-permute-start | bytes 1572872 | tf_op jit(solution)/shard_map/ppermute | solution.py:260
  200.0 10.6 %collective-permute-start.26 = (f32[1024,256]{1,0:T(8,128)}, f32[1024,256]{1,0:T(8,128)}, u32[]{:S(2)}, u32[]{:S(2)}) collective-permute-start(f32[1024,256]{1,0:T(8,128)} %get-tuple-element.18), channel_id=1, source_target_pairs={{0,8},{8,0},{16,24},{24,16},{1,9},{9,1},{17,25},{25,17},{2,10},{10... | collective-permute-start | bytes 3145736 | tf_op jit(solution)/shard_map/ppermute | solution.py:260
  202.9 34.1 %all-to-all-start.1 = ((f32[8,256,128]{2,1,0:T(8,128)}), f32[8,256,128]{2,1,0:T(8,128)S(1)}, u32[]{:S(2)}, u32[]{:S(2)}) async-start(f32[8,256,128]{2,1,0:T(8,128)} %gather_fusion.4), calls=%async_computation.1 | async-start | bytes 2097152 | tf_op jit(solution)/shard_map/all_to_all | solution.py:31
  211.6 14.1 %collective-permute-start.27 = (f32[1024,128]{1,0:T(8,128)S(1)}, f32[1024,128]{1,0:T(8,128)S(1)}, u32[]{:S(2)}, u32[]{:S(2)}) collective-permute-start(f32[1024,128]{1,0:T(8,128)S(1)} %slice_add_fusion.1), channel_id=1, source_target_pairs={{0,16},{8,24},{16,0},{24,8},{1,17},{9,25},{17,1},{25,9},{2,18},{10... | collective-permute-start | bytes 1572872 | tf_op jit(solution)/shard_map/ppermute | solution.py:260
  236.9 29.8 %all-to-all-start.2 = ((f32[8,256,128]{2,1,0:T(8,128)}), f32[8,256,128]{2,1,0:T(8,128)}, u32[]{:S(2)}, u32[]{:S(2)}) async-start(f32[8,256,128]{2,1,0:T(8,128)} %gather_fusion.10), calls=%async_computation.2 | async-start | bytes 2097152 | tf_op jit(solution)/shard_map/all_to_all | solution.py:31
  (29 other events, 382.6 us)

commit v2 on v1

--- a/solution.py
+++ b/solution.py
@@ -82,6 +82,74 @@
     return high, (value - high.astype(jnp.float32)).astype(jnp.bfloat16)
 
 
+def inbound_kernel(count, table, perm, tiles, energy, *rest):
+    homes, (out, buffer, semaphores) = rest[:count], rest[-3:]
+    slots, size, _ = buffer.shape
+
+    def copy(source, slot):
+        return pltpu.make_async_copy(source, buffer.at[slot], semaphores.at[slot])
+
+    for slot in range(slots):
+        if count == 1:
+            copy(homes[0].at[table[0, slot]], slot).start()
+        else:
+            for n, home in enumerate(homes):
+                pl.when(table[0, slot] == n)(lambda home=home: copy(home.at[0], slot).start())
+    orbital = lax.broadcasted_iota(jnp.int32, (size, size), 0)
+    for slot in range(slots):
+        sign = table[1, slot].astype(jnp.float32)
+        one_hot = jnp.where(perm[slot] == orbital, sign, 0.0).astype(jnp.bfloat16)
+        copy(homes[0].at[0], slot).wait()
+        values = buffer[slot]
+        high, _ = halves(values)
+        middle, low = halves(values - high.astype(jnp.float32))
+        moved = [
+            jnp.dot(one_hot, part, preferred_element_type=jnp.float32)
+            for part in (high, middle, low)
+        ]
+        sigma = moved[0] + moved[1] + moved[2] + energy[slot] * tiles[slot]
+        out[slot] = jnp.where(table[2, slot] > 0, sigma, 0.0)
+
+
+def inbound(table, perm, homes, tiles, energy, chunk, before):
+    slots, size, total = tiles.shape
+    width = homes[0].shape[2]
+
+    def here(n, table):
+        return (0, 0, chunk)
+
+    def whole(n, table):
+        return (0, 0, 0)
+
+    in_specs = [
+        pl.BlockSpec((slots, 1, size), whole),
+        pl.BlockSpec((slots, size, width), here),
+        pl.BlockSpec((slots, size, 1), whole),
+    ] + [pl.BlockSpec(memory_space=pl.ANY)] * len(homes)
+    operands = [table, perm[:, None, :], tiles, energy[:, :, None], *homes]
+    aliases = {}
+    if before is not None:
+        in_specs.append(pl.BlockSpec(memory_space=pl.ANY))
+        aliases = {len(operands): 0}
+        operands.append(before)
+    return pl.pallas_call(
+        functools.partial(inbound_kernel, len(homes)),
+        grid_spec=pltpu.PrefetchScalarGridSpec(
+            num_scalar_prefetch=1,
+            grid=(1,),
+            in_specs=in_specs,
+            out_specs=pl.BlockSpec((slots, size, width), here),
+            scratch_shapes=[
+                pltpu.VMEM((slots, size, width), jnp.float32),
+                pltpu.SemaphoreType.DMA((slots,)),
+            ],
+        ),
+        out_shape=jax.ShapeDtypeStruct((slots, size, total), jnp.float32),
+        input_output_aliases=aliases,
+        name="inbound",
+    )(*operands)
+
+
 def weights_kernel(index, weight, high, low):
     del index
     rows = weight.shape[0] * weight.shape[2]
@@ -244,26 +312,27 @@
     index = jnp.stack([line.sources()[n] * across + (x ^ mask) for n, mask in ways])
     turned = turned_weights(weights, index)
 
+    final_weight = lax.dynamic_slice_in_dim(weights, index[-1], 1, 1)
+    final_weight = final_weight.reshape(row_blocks * piece, interaction.shape[1])
+
+    def last_product(panel):
+        return lax.dot_general(
+            final_weight,
+            panel,
+            (((0,), (0,)), ((), ())),
+            precision=lax.Precision.HIGH,
+            preferred_element_type=jnp.float32,
+        )
+
     def product(panels):
         values = [panels[n][mask][0] for n, mask in ways]
-        total, first = None, 0
-        early = len(values) - max(1, len(values) // 4)
-        for name, size in (("a", early), ("c", len(values) - early)):
-            last = name == "c"
-            out = summed_products(
-                turned, first, values[first : first + size], total, 2 if last else 1,
-            )
-            total, first = out[0], first + size
-        return out
+        (total,) = summed_products(turned, 0, values[:-1], None, 1)
+        width = total.shape[1] // 2
+        sent = total[:, width:] + last_product(values[-1][:, width:])
+        return total[:, :width] + last_product(values[-1][:, :width]), sent
 
     def to_row(value, bit):
         return lax.ppermute(value, "row", xor_pairs(rows, bit))
-
-    def returned(home, tiles):
-        picked = jnp.take(home, source, axis=0, mode="clip")
-        back = jnp.einsum("sjp,sjn->spn", recouple, picked, precision=lax.Precision.HIGHEST)
-        sigma = back + particle_energy[:, :, None] * tiles
-        return jnp.where(is_live[:, None, None], sigma, 0.0)
 
     def halved(kept, arrived):
         width = kept.shape[1] // 2
@@ -271,8 +340,8 @@
 
     chunks = max(1, narrow // 128)
     step = narrow // chunks
-    tiles = [amplitudes[:, :, k * step : (k + 1) * step] for k in range(chunks)]
-    outs = []
+    sigma = None
+    live = is_live.astype(jnp.int32)
     panels, homes = [None] * chunks, [None] * chunks
     for k in range(chunks):
         shard = regroup(cut[:, :, k * step : (k + 1) * step])
@@ -291,11 +360,26 @@
         own = kept + arrived
         here = own.reshape(col_blocks, tile_rows, own.shape[1])
 
-        homes[k] = exchange(jnp.take(here, choice, axis=0, mode="clip"))
+        last = k + 1 == chunks
+        if last:
+            mine = jnp.take(here, jnp.take(choice, column ^ peers, mode="clip"), axis=0, mode="clip")
+            blocks = [mine[mask : mask + 1] for mask in range(columns)]
+            for mask in FARTHEST if columns == len(FARTHEST) + 1 else range(1, columns):
+                blocks[mask] = lax.ppermute(blocks[mask], "col", xor_pairs(columns, mask))
+            homes[k] = blocks
+        else:
+            homes[k] = [exchange(jnp.take(here, choice, axis=0, mode="clip"))]
         if k:
-            outs.append(returned(after(homes[k - 1], sent), tiles[k - 1]))
-    outs.append(returned(homes[-1], tiles[-1]))
-    return jnp.concatenate(outs, axis=2)
+            table = jnp.stack([source, own_phase, live])
+            homes[k - 1][0] = after(homes[k - 1][0], sent)
+            sigma = inbound(
+                table, own_perm, homes[k - 1], amplitudes, particle_energy, k - 1, sigma
+            )
+    table = jnp.stack([source ^ column, own_phase, live])
+    return inbound(table, own_perm, homes[-1], amplitudes, particle_energy, chunks - 1, sigma)
+
+
+FARTHEST = (6, 7, 4, 5, 2, 3, 1)
 
 
 def solution(mesh):

time: 274 us -> 286 us (1.044)
  waiting for transfers between devices: 130 us -> 136 us
  matrix products: 7.88 us -> 13.8 us
  starting transfers between devices: 59.9 us -> 55.8 us
  Pallas kernels: 42.2 us -> 46 us
    all_to_all x3 -> x2, waiting for transfers between devices: 63.1 us -> 36.7 us  [exchange(): return lax.all_to_all(tiles, 'col', split_axis=0, concat_axis=0, tiled=True)]
    ppermute x8, waiting for transfers between devices: 21.4 us -> 37.5 us  [across_x(): return lax.ppermute(held, 'col', links)]
    ppermute x0 -> x7, starting transfers between devices: none -> 12.3 us  [local(): blocks[mask] = lax.ppermute(blocks[mask], 'col', xor_pairs(columns, mask))]
    ppermute x10, starting transfers between devices: 24.3 us -> 12.2 us  [hop(): return lax.ppermute(value, 'col', links)]
    pallas_call x0 -> x2, Pallas kernels: none -> 11.6 us  [inbound(): pl.pallas_call(functools.partial(inbound_kernel, len(homes)), grid_spec=p...]
    ppermute x4, waiting for transfers between devices: 12.9 us -> 22.5 us  [to_row(): return lax.ppermute(value, 'row', xor_pairs(rows, bit))]
    pallas_call x4 -> x2, Pallas kernels: 28.3 us -> 20.4 us  [summed_products(): pl.pallas_call(functools.partial(product_kernel, count, start is not None...]
    all_to_all x3 -> x2, starting transfers between devices: 19.5 us -> 13.2 us  [exchange(): return lax.all_to_all(tiles, 'col', split_axis=0, concat_axis=0, tiled=True)]
  transfers between devices with their start and end apart: 31 -> 37, of which waited for: 14 -> 14; matrix products, arithmetic and copies ran while one was open for 9% -> 12% of each run, Pallas kernels for 16% -> 14%
where the time goes in v2:
time: 286 us; the launch traced here: 284 us
  waiting for transfers between devices  136 us (48%)
  starting transfers between devices  55.8 us (20%)
  Pallas kernels  46 us (16%)
  local copies, waits for them, and re-layouts  17.8 us (6%)
  matrix products  13.8 us (5%)
  other arithmetic  13.2 us (5%)
    ppermute x8, waiting for transfers between devices, across_x(): return lax.ppermute(held, 'col', links)  37.5 us
    all_to_all x2, waiting for transfers between devices, exchange(): return lax.all_to_all(tiles, 'col', split_axis=0, concat_axis=0, tiled=True)  36.7 us
    ppermute x10, waiting for transfers between devices, hop(): return lax.ppermute(value, 'col', links)  33 us
    ppermute x4, waiting for transfers between devices, to_row(): return lax.ppermute(value, 'row', xor_pairs(rows, bit))  22.5 us
    pallas_call x2, Pallas kernels, summed_products(): pl.pallas_call(functools.partial(product_kernel, count, start is not None...  20.4 us
    pallas_call x1, Pallas kernels, turned_weights(): pl.pallas_call(weights_kernel, grid_spec=pltpu.PrefetchScalarGridSpec(num...  14 us
    all_to_all x2, starting transfers between devices, exchange(): return lax.all_to_all(tiles, 'col', split_axis=0, concat_axis=0, tiled=True)  13.2 us
    ppermute x7, starting transfers between devices, local(): blocks[mask] = lax.ppermute(blocks[mask], 'col', xor_pairs(columns, mask))  12.3 us
  transfers between devices with their start and end apart: 37, of which 14 were waited for; matrix products, arithmetic and copies ran while one was open for 12% of the time, Pallas kernels for 14%

profile of v2, /device:TPU:0, one launch (start us, length us, event | category | flops | bytes accessed | tf_op | source)
XLA Modules:
  0.0 283.9 jit_solution(15295948816704217873)
XLA Ops:
  1.6 3.2 %fusion = f32[6,256,256]{2,1,0:T(8,128)S(1)} fusion(f32[6,256,256]{2,1,0:T(8,128)} %tiles.3, s32[6]{0:T(128)S(1)} %get-tuple-element.42, s32[6,256]{1,0:T(8,128)S(1)} %constant_dynamic-slice_fusion.1), kind=kOutput, calls=%fused_computation.12 | convolution fusion | flops 1209139200 | bytes 3151896 | tf_op jit(solution)/shard_map/sjp,spn->sjn/dot_general | solution.py:285
  6.0 7.4 %all-to-all-start = ((f32[8,6,32,256]{3,2,1,0:T(8,128)}), f32[8,6,32,256]{3,2,1,0:T(8,128)S(1)}, u32[]{:S(2)}, u32[]{:S(2)}) async-start(f32[8,6,32,256]{3,2,1,0:T(8,128)} %bitcast.37), calls=%async_computation | async-start | bytes 3145728 | tf_op jit(solution)/shard_map/all_to_all | solution.py:31
  13.7 36.7 %all-to-all-done = f32[8,6,32,256]{3,2,1,0:T(8,128)S(1)} async-done(((f32[8,6,32,256]{3,2,1,0:T(8,128)}), f32[8,6,32,256]{3,2,1,0:T(8,128)S(1)}, u32[]{:S(2)}, u32[]{:S(2)}) %all-to-all-start) | async-done | bytes 1572896 | tf_op jit(solution)/shard_map/all_to_all | solution.py:31
  69.7 6.7 %collective-permute-done.17.refs_15_ = f32[256,512]{1,0:T(8,128)} collective-permute-done((f32[256,512]{1,0:T(8,128)S(1)}, f32[256,512]{1,0:T(8,128)}, u32[]{:S(2)}, u32[]{:S(2)}) %collective-permute-start.17) | collective-permute-done | bytes 524320 | tf_op jit(solution)/shard_map/ppermute | solution.py:47
  79.2 8.5 %collective-permute-done.3.refs_15_ = f32[256,512]{1,0:T(8,128)} collective-permute-done((f32[256,512]{1,0:T(8,128)S(1)}, f32[256,512]{1,0:T(8,128)}, u32[]{:S(2)}, u32[]{:S(2)}) %collective-permute-start.3) | collective-permute-done | bytes 524320 | tf_op jit(solution)/shard_map/ppermute | solution.py:47
  90.4 14.0 %turned_weights.1 = (bf16[8,1024,256]{2,1,0:T(8,128)(2,1)}, bf16[8,1024,256]{2,1,0:T(8,128)(2,1)}) custom-call(s32[8]{0:T(128)} %stack.56.index, f32[8,8,32,1024]{3,2,1,0:T(8,128)} %bitcast.48), custom_call_target="tpu_custom_call" | custom-call | flops 4194304000 | bytes 16777216 | tf_op jit(solution)/shard_map/turned_weights/pallas_call | solution.py:164
  114.4 11.1 %collective-permute-done.23 = f32[256,512]{1,0:T(8,128)S(1)} collective-permute-done((f32[256,512]{1,0:T(8,128)}, f32[256,512]{1,0:T(8,128)S(1)}, u32[]{:S(2)}, u32[]{:S(2)}) %collective-permute-start.23) | collective-permute-done | bytes 524320 | tf_op jit(solution)/shard_map/ppermute | solution.py:47
  127.8 6.7 %collective-permute-done.9 = f32[256,512]{1,0:T(8,128)S(1)} collective-permute-done((f32[256,512]{1,0:T(8,128)}, f32[256,512]{1,0:T(8,128)S(1)}, u32[]{:S(2)}, u32[]{:S(2)}) %collective-permute-start.9) | collective-permute-done | bytes 524320 | tf_op jit(solution)/shard_map/ppermute | solution.py:47
  137.5 5.5 %collective-permute-done.21.refs_18_ = f32[256,512]{1,0:T(8,128)S(1)} collective-permute-done((f32[256,512]{1,0:T(8,128)}, f32[256,512]{1,0:T(8,128)S(1)}, u32[]{:S(2)}, u32[]{:S(2)}) %collective-permute-start.21) | collective-permute-done | bytes 524320 | tf_op jit(solution)/shard_map/ppermute | solution.py:302
  144.5 9.8 %collective-permute-done.24.refs_20_ = f32[256,512]{1,0:T(8,128)S(1)} collective-permute-done((f32[256,512]{1,0:T(8,128)S(1)}, f32[256,512]{1,0:T(8,128)S(1)}, u32[]{:S(2)}, u32[]{:S(2)}) %collective-permute-start.24) | collective-permute-done | bytes 524320 | tf_op jit(solution)/shard_map/ppermute | solution.py:302
  155.7 10.2 %summed_products.3 = f32[1024,512]{1,0:T(8,128)} custom-call(bf16[8,1024,256]{2,1,0:T(8,128)(2,1)} %get-tuple-element.9.refs_0_.refs_1_.refs_2_.refs_3_.refs_4_.refs_5_.refs_6_, bf16[8,1024,256]{2,1,0:T(8,128)(2,1)} %get-tuple-element.9.refs_0_.refs_1_.refs_2_.refs_3_.refs_4_.refs_5_.refs_6_, ...), custom_call_target="tpu_custom_call" | custom-call | flops 5637144576 | bytes 15204352 | tf_op jit(solution)/shard_map/summed_products/pallas_call | solution.py:221
  165.9 22.2 %collective-permute-done.25 = f32[256,512]{1,0:T(8,128)} collective-permute-done((f32[256,512]{1,0:T(8,128)}, f32[256,512]{1,0:T(8,128)}, u32[]{:S(2)}, u32[]{:S(2)}) %collective-permute-start.25) | collective-permute-done | bytes 524320 | tf_op jit(solution)/shard_map/ppermute | solution.py:302
  188.1 3.3 %slice_add_fusion = f32[1024,256]{1,0:T(8,128)} fusion(f32[1024,512]{1,0:T(8,128)} %summed_products.3, f32[256,1024]{1,0:T(8,128)S(1)} %bitcast.38, f32[256,512]{1,0:T(8,128)} %collective-permute-done.25), kind=kOutput, calls=%fused_computation.16 | convolution fusion | flops 402915328 | bytes 3407872 | tf_op jit(solution)/shard_map/dot_general | solution.py:319
  192.2 10.2 %summed_products.2 = f32[1024,512]{1,0:T(8,128)} custom-call(bf16[8,1024,256]{2,1,0:T(8,128)(2,1)} %get-tuple-element.9.refs_0_.refs_1_.refs_2_.refs_3_.refs_4_.refs_5_.refs_6_, bf16[8,1024,256]{2,1,0:T(8,128)(2,1)} %get-tuple-element.9.refs_0_.refs_1_.refs_2_.refs_3_.refs_4_.refs_5_.refs_6_, ...), custom_call_target="tpu_custom_call" | custom-call | flops 5637144576 | bytes 15204352 | tf_op jit(solution)/shard_map/summed_products/pallas_call | solution.py:221
  202.5 3.4 %slice_add_fusion.2 = f32[1024,256]{1,0:T(8,128)} fusion(f32[1024,512]{1,0:T(8,128)} %summed_products.2, f32[256,1024]{1,0:T(8,128)S(1)} %bitcast.39, f32[256,512]{1,0:T(8,128)S(1)} %collective-permute-done.11), kind=kOutput, calls=%fused_computation.18 | convolution fusion | flops 402915328 | bytes 3407872 | tf_op jit(solution)/shard_map/dot_general | solution.py:319
  211.4 12.0 %collective-permute-done.27 = f32[1024,128]{1,0:T(8,128)S(1)} collective-permute-done((f32[1024,128]{1,0:T(8,128)S(1)}, f32[1024,128]{1,0:T(8,128)S(1)}, u32[]{:S(2)}, u32[]{:S(2)}) %collective-permute-start.27) | collective-permute-done | bytes 524320 | tf_op jit(solution)/shard_map/ppermute | solution.py:335
  226.1 5.7 %all-to-all-start.1 = ((f32[8,256,128]{2,1,0:T(8,128)}), f32[8,256,128]{2,1,0:T(8,128)}, u32[]{:S(2)}, u32[]{:S(2)}) async-start(f32[8,256,128]{2,1,0:T(8,128)} %gather_fusion.10), calls=%async_computation.1 | async-start | bytes 2097152 | tf_op jit(solution)/shard_map/all_to_all | solution.py:31
  238.2 10.5 %collective-permute-done.13 = f32[1024,128]{1,0:T(8,128)S(1)} collective-permute-done((f32[1024,128]{1,0:T(8,128)S(1)}, f32[1024,128]{1,0:T(8,128)S(1)}, u32[]{:S(2)}, u32[]{:S(2)}) %collective-permute-start.13) | collective-permute-done | bytes 524320 | tf_op jit(solution)/shard_map/ppermute | solution.py:335
  253.1 2.2 collective-permute-start.29
  255.9 2.6 collective-permute-start.31
  259.7 3.1 %collective-permute-start.33 = (f32[1,256,128]{2,1,0:T(8,128)S(1)}, f32[1,256,128]{2,1,0:T(8,128)S(1)}, u32[]{:S(2)}, u32[]{:S(2)}) collective-permute-start(f32[1,256,128]{2,1,0:T(8,128)S(1)} %get-tuple-element.33), channel_id=1, source_target_pairs={{0,6},{1,7},{2,4},{3,5},{4,2},{5,3},{6,0},{7,1},{8,14},{9,15},{10,... | collective-permute-start | bytes 393224 | tf_op jit(solution)/shard_map/ppermute | solution.py:368
  268.7 5.8 %inbound.2.rest_8_ = f32[6,256,256]{2,1,0:T(8,128)} custom-call(s32[3,6]{1,0:T(4,128)} %get-tuple-element.40.table, s32[6,1,256]{2,1,0:T(1,128)} %broadcast_in_dim.126.perm, f32[6,256,256]{2,1,0:T(8,128)} %tiles.3, f32[6,256,1]{2,1,0:T(8,128)} %copy.14.energy, f32[8,256,128]{2,1,0:T(8,128)} %all-to-all-done.1.rest_0_), custom_call_target="tpu_custom_call" | custom-call | tf_op jit(solution)/shard_map/inbound/pallas_call | solution.py:135
  274.6 2.5 collective-permute-done.32.rest_5_
  277.9 5.8 %inbound.3 = f32[6,256,256]{2,1,0:T(8,128)} custom-call(s32[3,6]{1,0:T(4,128)} %get-tuple-element.41.table, s32[6,1,256]{2,1,0:T(1,128)} %broadcast_in_dim.126.perm, f32[6,256,256]{2,1,0:T(8,128)} %tiles.3, f32[6,256,1]{2,1,0:T(8,128)} %copy.14.energy, f32[1,256,128]{2,1,0:T(8,128)} %get-tuple-element.39.rest_0_, ...), custom_call_target="tpu_custom_call", output_to_operand_aliasing={{}: (12, {})} | custom-call | tf_op jit(solution)/shard_map/inbound/pallas_call | solution.py:135
  (158 shorter events, 73.8 us)
Async XLA Ops:
  6.0 44.4 %all-to-all-start = ((f32[8,6,32,256]{3,2,1,0:T(8,128)}), f32[8,6,32,256]{3,2,1,0:T(8,128)S(1)}, u32[]{:S(2)}, u32[]{:S(2)}) async-start(f32[8,6,32,256]{3,2,1,0:T(8,128)} %bitcast.37), calls=%async_computation | async-start | bytes 3145728 | tf_op jit(solution)/shard_map/all_to_all | solution.py:31
  65.9 21.8 %collective-permute-start.3 = (f32[256,512]{1,0:T(8,128)S(1)}, f32[256,512]{1,0:T(8,128)}, u32[]{:S(2)}, u32[]{:S(2)}) collective-permute-start(f32[256,512]{1,0:T(8,128)S(1)} %pad_maximum_fusion.refs_14_), channel_id=1, source_target_pairs={{0,2},{1,3},{2,0},{3,1},{4,6},{5,7},{6,4},{7,5},{8,10},{9,11},{10,... | collective-permute-start | bytes 1572872 | tf_op jit(solution)/shard_map/ppermute | solution.py:47
  67.7 21.4 %collective-permute-start.5 = (f32[256,512]{1,0:T(8,128)S(1)}, f32[256,512]{1,0:T(8,128)}, u32[]{:S(2)}, u32[]{:S(2)}) collective-permute-start(f32[256,512]{1,0:T(8,128)S(1)} %pad_maximum_fusion.refs_14_), channel_id=1, source_target_pairs={{2,4},{3,5},{4,2},{5,3},{10,12},{11,13},{12,10},{13,11},{18,20},{1... | collective-permute-start | bytes 1572872 | tf_op jit(solution)/shard_map/ppermute | solution.py:47
  76.4 30.8 %collective-permute-start.22 = (f32[256,512]{1,0:T(8,128)}, f32[256,512]{1,0:T(8,128)}, u32[]{:S(2)}, u32[]{:S(2)}) collective-permute-start(f32[256,512]{1,0:T(8,128)} %collective-permute-done.17.refs_15_), channel_id=1, source_target_pairs={{2,4},{3,5},{4,2},{5,3},{10,12},{11,13},{12,10},{13,11},{18,20},{1... | collective-permute-start | bytes 1572872 | tf_op jit(solution)/shard_map/ppermute | solution.py:47
  77.9 29.9 %collective-permute-start.20 = (f32[256,512]{1,0:T(8,128)S(1)}, f32[256,512]{1,0:T(8,128)}, u32[]{:S(2)}, u32[]{:S(2)}) collective-permute-start(f32[256,512]{1,0:T(8,128)S(1)} %collective-permute-done.19), channel_id=1, source_target_pairs={{2,0},{3,1},{4,6},{5,7},{10,8},{11,9},{12,14},{13,15},{18,16},{19,... | collective-permute-start | bytes 1572872 | tf_op jit(solution)/shard_map/ppermute | solution.py:47
  87.6 22.6 %collective-permute-start.8 = (f32[256,512]{1,0:T(8,128)}, f32[256,512]{1,0:T(8,128)}, u32[]{:S(2)}, u32[]{:S(2)}) collective-permute-start(f32[256,512]{1,0:T(8,128)} %collective-permute-done.3.refs_15_), channel_id=1, source_target_pairs={{2,4},{3,5},{4,2},{5,3},{10,12},{11,13},{12,10},{13,11},{18,20},{1... | collective-permute-start | bytes 1572872 | tf_op jit(solution)/shard_map/ppermute | solution.py:47
  89.1 22.6 %collective-permute-start.6 = (f32[256,512]{1,0:T(8,128)}, f32[256,512]{1,0:T(8,128)}, u32[]{:S(2)}, u32[]{:S(2)}) collective-permute-start(f32[256,512]{1,0:T(8,128)} %collective-permute-done.5), channel_id=1, source_target_pairs={{2,0},{3,1},{4,6},{5,7},{10,8},{11,9},{12,14},{13,15},{18,16},{19,... | collective-permute-start | bytes 1572872 | tf_op jit(solution)/shard_map/ppermute | solution.py:47
  105.7 31.2 %collective-permute-start.18 = (f32[256,512]{1,0:T(8,128)S(1)}, f32[256,512]{1,0:T(8,128)S(1)}, u32[]{:S(2)}, u32[]{:S(2)}) collective-permute-start(f32[256,512]{1,0:T(8,128)S(1)} %pad_maximum_fusion.1.refs_14_), channel_id=1, source_target_pairs={{0,1},{1,0},{2,3},{3,2},{4,5},{5,4},{6,7},{7,6},{8,9},{9,8},{10,11... | collective-permute-start | bytes 1572872 | tf_op jit(solution)/shard_map/ppermute | solution.py:302
  107.2 84.2 %collective-permute-start.4 = (f32[256,512]{1,0:T(8,128)S(1)}, f32[256,512]{1,0:T(8,128)}, u32[]{:S(2)}, u32[]{:S(2)}) collective-permute-start(f32[256,512]{1,0:T(8,128)S(1)} %pad_maximum_fusion.refs_14_), channel_id=1, source_target_pairs={{0,1},{1,0},{2,3},{3,2},{4,5},{5,4},{6,7},{7,6},{8,9},{9,8},{10,11... | collective-permute-start | bytes 1572872 | tf_op jit(solution)/shard_map/ppermute | solution.py:302
  107.8 17.7 %collective-permute-start.23 = (f32[256,512]{1,0:T(8,128)}, f32[256,512]{1,0:T(8,128)S(1)}, u32[]{:S(2)}, u32[]{:S(2)}) collective-permute-start(f32[256,512]{1,0:T(8,128)} %collective-permute-done.22), channel_id=1, source_target_pairs={{2,0},{3,1},{4,6},{5,7},{10,8},{11,9},{12,14},{13,15},{18,16},{19,... | collective-permute-start | bytes 1572872 | tf_op jit(solution)/shard_map/ppermute | solution.py:47
  110.2 32.8 %collective-permute-start.21 = (f32[256,512]{1,0:T(8,128)}, f32[256,512]{1,0:T(8,128)S(1)}, u32[]{:S(2)}, u32[]{:S(2)}) collective-permute-start(f32[256,512]{1,0:T(8,128)} %collective-permute-done.17.refs_15_), channel_id=1, source_target_pairs={{0,1},{1,0},{2,3},{3,2},{4,5},{5,4},{6,7},{7,6},{8,9},{9,8},{10,11... | collective-permute-start | bytes 1572872 | tf_op jit(solution)/shard_map/ppermute | solution.py:302
  111.7 22.8 %collective-permute-start.9 = (f32[256,512]{1,0:T(8,128)}, f32[256,512]{1,0:T(8,128)S(1)}, u32[]{:S(2)}, u32[]{:S(2)}) collective-permute-start(f32[256,512]{1,0:T(8,128)} %collective-permute-done.8), channel_id=1, source_target_pairs={{2,0},{3,1},{4,6},{5,7},{10,8},{11,9},{12,14},{13,15},{18,16},{19,... | collective-permute-start | bytes 1572872 | tf_op jit(solution)/shard_map/ppermute | solution.py:47
  125.5 28.8 %collective-permute-start.24 = (f32[256,512]{1,0:T(8,128)S(1)}, f32[256,512]{1,0:T(8,128)S(1)}, u32[]{:S(2)}, u32[]{:S(2)}) collective-permute-start(f32[256,512]{1,0:T(8,128)S(1)} %broadcast_select_fusion.1.refs_17_), channel_id=1, source_target_pairs={{0,1},{1,0},{2,3},{3,2},{4,5},{5,4},{6,7},{7,6},{8,9},{9,8},{10,11... | collective-permute-start | bytes 1572872 | tf_op jit(solution)/shard_map/ppermute | solution.py:302
  134.5 56.8 %collective-permute-start.7 = (f32[256,512]{1,0:T(8,128)}, f32[256,512]{1,0:T(8,128)}, u32[]{:S(2)}, u32[]{:S(2)}) collective-permute-start(f32[256,512]{1,0:T(8,128)} %collective-permute-done.3.refs_15_), channel_id=1, source_target_pairs={{0,1},{1,0},{2,3},{3,2},{4,5},{5,4},{6,7},{7,6},{8,9},{9,8},{10,11... | collective-permute-start | bytes 1572872 | tf_op jit(solution)/shard_map/ppermute | solution.py:302
  136.9 54.5 %collective-permute-start.10 = (f32[256,512]{1,0:T(8,128)S(1)}, f32[256,512]{1,0:T(8,128)S(1)}, u32[]{:S(2)}, u32[]{:S(2)}) collective-permute-start(f32[256,512]{1,0:T(8,128)S(1)} %broadcast_select_fusion.3.refs_17_), channel_id=1, source_target_pairs={{0,1},{1,0},{2,3},{3,2},{4,5},{5,4},{6,7},{7,6},{8,9},{9,8},{10,11... | collective-permute-start | bytes 1572872 | tf_op jit(solution)/shard_map/ppermute | solution.py:302
  143.0 45.0 %collective-permute-start.25 = (f32[256,512]{1,0:T(8,128)}, f32[256,512]{1,0:T(8,128)}, u32[]{:S(2)}, u32[]{:S(2)}) collective-permute-start(f32[256,512]{1,0:T(8,128)} %broadcast_select_fusion.refs_19_), channel_id=1, source_target_pairs={{0,1},{1,0},{2,3},{3,2},{4,5},{5,4},{6,7},{7,6},{8,9},{9,8},{10,11... | collective-permute-start | bytes 1572872 | tf_op jit(solution)/shard_map/ppermute | solution.py:302
  154.3 48.2 %collective-permute-start.11 = (f32[256,512]{1,0:T(8,128)}, f32[256,512]{1,0:T(8,128)S(1)}, u32[]{:S(2)}, u32[]{:S(2)}) collective-permute-start(f32[256,512]{1,0:T(8,128)} %broadcast_select_fusion.2.refs_19_), channel_id=1, source_target_pairs={{0,1},{1,0},{2,3},{3,2},{4,5},{5,4},{6,7},{7,6},{8,9},{9,8},{10,11... | collective-permute-start | bytes 1572872 | tf_op jit(solution)/shard_map/ppermute | solution.py:302
  191.4 17.0 %collective-permute-start.26 = (f32[1024,256]{1,0:T(8,128)}, f32[1024,256]{1,0:T(8,128)}, u32[]{:S(2)}, u32[]{:S(2)}) collective-permute-start(f32[1024,256]{1,0:T(8,128)} %slice_add_fusion), channel_id=1, source_target_pairs={{0,8},{8,0},{16,24},{24,16},{1,9},{9,1},{17,25},{25,17},{2,10},{10... | collective-permute-start | bytes 3145736 | tf_op jit(solution)/shard_map/ppermute | solution.py:335
  205.9 27.9 %collective-permute-start.12 = (f32[1024,256]{1,0:T(8,128)}, f32[1024,256]{1,0:T(8,128)}, u32[]{:S(2)}, u32[]{:S(2)}) collective-permute-start(f32[1024,256]{1,0:T(8,128)} %slice_add_fusion.2), channel_id=1, source_target_pairs={{0,8},{8,0},{16,24},{24,16},{1,9},{9,1},{17,25},{25,17},{2,10},{10... | collective-permute-start | bytes 3145736 | tf_op jit(solution)/shard_map/ppermute | solution.py:335
  226.1 42.6 %all-to-all-start.1 = ((f32[8,256,128]{2,1,0:T(8,128)}), f32[8,256,128]{2,1,0:T(8,128)}, u32[]{:S(2)}, u32[]{:S(2)}) async-start(f32[8,256,128]{2,1,0:T(8,128)} %gather_fusion.10), calls=%async_computation.1 | async-start | bytes 2097152 | tf_op jit(solution)/shard_map/all_to_all | solution.py:31
  255.9 18.7 %collective-permute-start.30 = (f32[1,256,128]{2,1,0:T(8,128)S(1)}, f32[1,256,128]{2,1,0:T(8,128)S(1)}, u32[]{:S(2)}, u32[]{:S(2)}) collective-permute-start(f32[1,256,128]{2,1,0:T(8,128)S(1)} %get-tuple-element.36), channel_id=1, source_target_pairs={{0,3},{1,2},{2,1},{3,0},{4,7},{5,6},{6,5},{7,4},{8,11},{9,10},{10,... | collective-permute-start | bytes 393224 | tf_op jit(solution)/shard_map/ppermute | solution.py:368
  255.9 18.7 %collective-permute-start.31 = (f32[1,256,128]{2,1,0:T(8,128)S(1)}, f32[1,256,128]{2,1,0:T(8,128)S(1)}, u32[]{:S(2)}, u32[]{:S(2)}) collective-permute-start(f32[1,256,128]{2,1,0:T(8,128)S(1)} %get-tuple-element.35), channel_id=1, source_target_pairs={{0,4},{1,5},{2,6},{3,7},{4,0},{5,1},{6,2},{7,3},{8,12},{9,13},{10,... | collective-permute-start | bytes 393224 | tf_op jit(solution)/shard_map/ppermute | solution.py:368
  258.6 18.5 %collective-permute-start.32 = (f32[1,256,128]{2,1,0:T(8,128)S(1)}, f32[1,256,128]{2,1,0:T(8,128)S(1)}, u32[]{:S(2)}, u32[]{:S(2)}) collective-permute-start(f32[1,256,128]{2,1,0:T(8,128)S(1)} %get-tuple-element.34), channel_id=1, source_target_pairs={{0,5},{1,4},{2,7},{3,6},{4,1},{5,0},{6,3},{7,2},{8,13},{9,12},{10,... | collective-permute-start | bytes 393224 | tf_op jit(solution)/shard_map/ppermute | solution.py:368
  259.7 17.4 %collective-permute-start.33 = (f32[1,256,128]{2,1,0:T(8,128)S(1)}, f32[1,256,128]{2,1,0:T(8,128)S(1)}, u32[]{:S(2)}, u32[]{:S(2)}) collective-permute-start(f32[1,256,128]{2,1,0:T(8,128)S(1)} %get-tuple-element.33), channel_id=1, source_target_pairs={{0,6},{1,7},{2,4},{3,5},{4,2},{5,3},{6,0},{7,1},{8,14},{9,15},{10,... | collective-permute-start | bytes 393224 | tf_op jit(solution)/shard_map/ppermute | solution.py:368
  (38 other events, 382.4 us)

commit v3 on v2

--- a/solution.py
+++ b/solution.py
@@ -324,9 +324,11 @@
             preferred_element_type=jnp.float32,
         )
 
-    def product(panels):
+    def product(panels, chunk):
         values = [panels[n][mask][0] for n, mask in ways]
-        (total,) = summed_products(turned, 0, values[:-1], None, 1)
+        early = len(values) // 2 - chunk
+        (total,) = summed_products(turned, 0, values[:early], None, 1)
+        (total,) = summed_products(turned, early, values[early:-1], total, 1)
         width = total.shape[1] // 2
         sent = total[:, width:] + last_product(values[-1][:, width:])
         return total[:, :width] + last_product(values[-1][:, :width]), sent
@@ -347,7 +349,7 @@
         shard = regroup(cut[:, :, k * step : (k + 1) * step])
         panels[k] = crossed(line.gather(shard))
     for k in range(chunks):
-        kept, sent = product(panels[k])
+        kept, sent = product(panels[k], k)
         bit = 1
         while True:
             arrived = to_row(sent, bit)

time: 286 us -> 258 us (0.902)
  waiting for transfers between devices: 136 us -> 104 us
  Pallas kernels: 46 us -> 52.3 us
    ppermute x8, waiting for transfers between devices: 37.5 us -> 8.87 us  [across_x(): return lax.ppermute(held, 'col', links)]
    ppermute x10, waiting for transfers between devices: 33 us -> 24.1 us  [hop(): return lax.ppermute(value, 'col', links)]
    pallas_call x2 -> x4, Pallas kernels: 20.4 us -> 26.7 us  [summed_products(): pl.pallas_call(functools.partial(product_kernel, count, start is not None...]
    ppermute x6, waiting for transfers between devices: 2.7 us -> 6.06 us  [regroup(): part = lax.ppermute(part, 'row', xor_pairs(rows, mask))]
  transfers between devices with their start and end apart: 37 -> 37, of which waited for: 14 -> 15; matrix products, arithmetic and copies ran while one was open for 12% -> 13% of each run, Pallas kernels for 14% -> 18%
where the time goes in v3:
time: 258 us; the launch traced here: 256 us
  waiting for transfers between devices  104 us (40%)
  starting transfers between devices  56.6 us (22%)
  Pallas kernels  52.3 us (20%)
  local copies, waits for them, and re-layouts  17.1 us (7%)
  matrix products  13.8 us (5%)
  other arithmetic  11.3 us (4%)
    all_to_all x2, waiting for transfers between devices, exchange(): return lax.all_to_all(tiles, 'col', split_axis=0, concat_axis=0, tiled=True)  36.7 us
    pallas_call x4, Pallas kernels, summed_products(): pl.pallas_call(functools.partial(product_kernel, count, start is not None...  26.7 us
    ppermute x4, waiting for transfers between devices, to_row(): return lax.ppermute(value, 'row', xor_pairs(rows, bit))  25.1 us
    ppermute x10, waiting for transfers between devices, hop(): return lax.ppermute(value, 'col', links)  24.1 us
    all_to_all x2, starting transfers between devices, exchange(): return lax.all_to_all(tiles, 'col', split_axis=0, concat_axis=0, tiled=True)  14.5 us
    pallas_call x1, Pallas kernels, turned_weights(): pl.pallas_call(weights_kernel, grid_spec=pltpu.PrefetchScalarGridSpec(num...  14 us
    ppermute x7, starting transfers between devices, local(): blocks[mask] = lax.ppermute(blocks[mask], 'col', xor_pairs(columns, mask))  13.2 us
    ppermute x10, starting transfers between devices, hop(): return lax.ppermute(value, 'col', links)  12.8 us
  transfers between devices with their start and end apart: 37, of which 15 were waited for; matrix products, arithmetic and copies ran while one was open for 13% of the time, Pallas kernels for 18%

profile of v3, /device:TPU:0, one launch (start us, length us, event | category | flops | bytes accessed | tf_op | source)
XLA Modules:
  0.0 256.2 jit_solution(15272515313232852329)
XLA Ops:
  1.6 3.2 %fusion = f32[6,256,256]{2,1,0:T(8,128)S(1)} fusion(f32[6,256,256]{2,1,0:T(8,128)} %tiles.3, s32[6]{0:T(128)S(1)} %get-tuple-element.42, s32[6,256]{1,0:T(8,128)S(1)} %constant_dynamic-slice_fusion.1), kind=kOutput, calls=%fused_computation.12 | convolution fusion | flops 1209139200 | bytes 3151896 | tf_op jit(solution)/shard_map/sjp,spn->sjn/dot_general | solution.py:285
  6.0 7.4 %all-to-all-start = ((f32[8,6,32,256]{3,2,1,0:T(8,128)}), f32[8,6,32,256]{3,2,1,0:T(8,128)S(1)}, u32[]{:S(2)}, u32[]{:S(2)}) async-start(f32[8,6,32,256]{3,2,1,0:T(8,128)} %bitcast.37), calls=%async_computation | async-start | bytes 3145728 | tf_op jit(solution)/shard_map/all_to_all | solution.py:31
  13.7 36.7 %all-to-all-done = f32[8,6,32,256]{3,2,1,0:T(8,128)S(1)} async-done(((f32[8,6,32,256]{3,2,1,0:T(8,128)}), f32[8,6,32,256]{3,2,1,0:T(8,128)S(1)}, u32[]{:S(2)}, u32[]{:S(2)}) %all-to-all-start) | async-done | bytes 1572896 | tf_op jit(solution)/shard_map/all_to_all | solution.py:31
  56.2 2.9 %collective-permute-done.16 = f32[8,32,128]{2,1,0:T(8,128)S(1)} collective-permute-done((f32[8,32,128]{2,1,0:T(8,128)S(1)}, f32[8,32,128]{2,1,0:T(8,128)S(1)}, u32[]{:S(2)}, u32[]{:S(2)}) %collective-permute-start.16) | collective-permute-done | bytes 131104 | tf_op jit(solution)/shard_map/ppermute | solution.py:294
  76.3 14.0 %turned_weights.1 = (bf16[8,1024,256]{2,1,0:T(8,128)(2,1)}, bf16[8,1024,256]{2,1,0:T(8,128)(2,1)}) custom-call(s32[8]{0:T(128)} %stack.56.index, f32[8,8,32,1024]{3,2,1,0:T(8,128)} %bitcast.48), custom_call_target="tpu_custom_call" | custom-call | flops 4194304000 | bytes 16777216 | tf_op jit(solution)/shard_map/turned_weights/pallas_call | solution.py:164
  93.2 3.7 %collective-permute-done.22 = f32[256,512]{1,0:T(8,128)} collective-permute-done((f32[256,512]{1,0:T(8,128)S(1)}, f32[256,512]{1,0:T(8,128)}, u32[]{:S(2)}, u32[]{:S(2)}) %collective-permute-start.22) | collective-permute-done | bytes 524320 | tf_op jit(solution)/shard_map/ppermute | solution.py:47
  104.3 7.2 %summed_products.6.refs_9_ = f32[1024,512]{1,0:T(8,128)} custom-call(bf16[8,1024,256]{2,1,0:T(8,128)(2,1)} %get-tuple-element.9.refs_0_.refs_1_.refs_2_.refs_3_, bf16[8,1024,256]{2,1,0:T(8,128)(2,1)} %get-tuple-element.9.refs_0_.refs_1_.refs_2_.refs_3_, bf16[8,1024,256]{2,1,0:T(8,128)(2,1)} %get-tuple-element.9.refs_0_.refs_1_.refs_2_.refs_3_, ...), custom_call_target="tpu_custom_call" | custom-call | flops 3221225472 | bytes 10485760 | tf_op jit(solution)/shard_map/summed_products/pallas_call | solution.py:221
  112.1 3.2 %collective-permute-done.20 = f32[256,512]{1,0:T(8,128)} collective-permute-done((f32[256,512]{1,0:T(8,128)}, f32[256,512]{1,0:T(8,128)}, u32[]{:S(2)}, u32[]{:S(2)}) %collective-permute-start.20) | collective-permute-done | bytes 524320 | tf_op jit(solution)/shard_map/ppermute | solution.py:47
  118.8 7.7 %collective-permute-done.4 = f32[256,512]{1,0:T(8,128)S(1)} collective-permute-done((f32[256,512]{1,0:T(8,128)}, f32[256,512]{1,0:T(8,128)S(1)}, u32[]{:S(2)}, u32[]{:S(2)}) %collective-permute-start.4) | collective-permute-done | bytes 524320 | tf_op jit(solution)/shard_map/ppermute | solution.py:47
  128.0 8.4 %collective-permute-done.8 = f32[256,512]{1,0:T(8,128)S(1)} collective-permute-done((f32[256,512]{1,0:T(8,128)}, f32[256,512]{1,0:T(8,128)S(1)}, u32[]{:S(2)}, u32[]{:S(2)}) %collective-permute-start.8) | collective-permute-done | bytes 524320 | tf_op jit(solution)/shard_map/ppermute | solution.py:47
  140.8 6.2 %summed_products.7 = f32[1024,512]{1,0:T(8,128)} custom-call(bf16[8,1024,256]{2,1,0:T(8,128)(2,1)} %get-tuple-element.9.refs_0_.refs_1_.refs_2_.refs_3_, bf16[8,1024,256]{2,1,0:T(8,128)(2,1)} %get-tuple-element.9.refs_0_.refs_1_.refs_2_.refs_3_, bf16[8,1024,256]{2,1,0:T(8,128)(2,1)} %get-tuple-element.9.refs_0_.refs_1_.refs_2_.refs_3_, ...), custom_call_target="tpu_custom_call" | custom-call | flops 2415919104 | bytes 8912896 | tf_op jit(solution)/shard_map/summed_products/pallas_call | solution.py:221
  147.0 3.3 %slice_add_fusion = f32[1024,256]{1,0:T(8,128)} fusion(f32[1024,512]{1,0:T(8,128)} %summed_products.7, f32[256,1024]{1,0:T(8,128)S(1)} %bitcast.38, f32[256,512]{1,0:T(8,128)} %collective-permute-done.25), kind=kOutput, calls=%fused_computation.16 | convolution fusion | flops 402915328 | bytes 3407872 | tf_op jit(solution)/shard_map/dot_general | solution.py:319
  150.4 5.8 %summed_products.4.refs_12_ = f32[1024,512]{1,0:T(8,128)} custom-call(bf16[8,1024,256]{2,1,0:T(8,128)(2,1)} %get-tuple-element.9.refs_0_.refs_1_.refs_2_.refs_3_, bf16[8,1024,256]{2,1,0:T(8,128)(2,1)} %get-tuple-element.9.refs_0_.refs_1_.refs_2_.refs_3_, bf16[8,1024,256]{2,1,0:T(8,128)(2,1)} %get-tuple-element.9.refs_0_.refs_1_.refs_2_.refs_3_, ...), custom_call_target="tpu_custom_call" | custom-call | flops 2415919104 | bytes 8912896 | tf_op jit(solution)/shard_map/summed_products/pallas_call | solution.py:221
  156.2 6.5 %collective-permute-done.9.refs_11_ = f32[256,512]{1,0:T(8,128)} collective-permute-done((f32[256,512]{1,0:T(8,128)S(1)}, f32[256,512]{1,0:T(8,128)}, u32[]{:S(2)}, u32[]{:S(2)}) %collective-permute-start.9) | collective-permute-done | bytes 524320 | tf_op jit(solution)/shard_map/ppermute | solution.py:302
  162.7 7.5 %summed_products.5 = f32[1024,512]{1,0:T(8,128)} custom-call(bf16[8,1024,256]{2,1,0:T(8,128)(2,1)} %get-tuple-element.9.refs_0_.refs_1_.refs_2_.refs_3_, bf16[8,1024,256]{2,1,0:T(8,128)(2,1)} %get-tuple-element.9.refs_0_.refs_1_.refs_2_.refs_3_, bf16[8,1024,256]{2,1,0:T(8,128)(2,1)} %get-tuple-element.9.refs_0_.refs_1_.refs_2_.refs_3_, ...), custom_call_target="tpu_custom_call" | custom-call | flops 3221225472 | bytes 10485760 | tf_op jit(solution)/shard_map/summed_products/pallas_call | solution.py:221
  172.6 3.4 %slice_add_fusion.2 = f32[1024,256]{1,0:T(8,128)} fusion(f32[1024,512]{1,0:T(8,128)} %summed_products.5, f32[256,1024]{1,0:T(8,128)S(1)} %bitcast.39, f32[256,512]{1,0:T(8,128)S(1)} %collective-permute-done.11), kind=kOutput, calls=%fused_computation.18 | convolution fusion | flops 402915328 | bytes 3407872 | tf_op jit(solution)/shard_map/dot_general | solution.py:319
  180.1 13.3 %collective-permute-done.27 = f32[1024,128]{1,0:T(8,128)S(1)} collective-permute-done((f32[1024,128]{1,0:T(8,128)S(1)}, f32[1024,128]{1,0:T(8,128)S(1)}, u32[]{:S(2)}, u32[]{:S(2)}) %collective-permute-start.27) | collective-permute-done | bytes 524320 | tf_op jit(solution)/shard_map/ppermute | solution.py:337
  196.2 7.1 %all-to-all-start.1 = ((f32[8,256,128]{2,1,0:T(8,128)}), f32[8,256,128]{2,1,0:T(8,128)}, u32[]{:S(2)}, u32[]{:S(2)}) async-start(f32[8,256,128]{2,1,0:T(8,128)} %gather_fusion.10), calls=%async_computation.1 | async-start | bytes 2097152 | tf_op jit(solution)/shard_map/all_to_all | solution.py:31
  208.7 11.8 %collective-permute-done.13 = f32[1024,128]{1,0:T(8,128)S(1)} collective-permute-done((f32[1024,128]{1,0:T(8,128)S(1)}, f32[1024,128]{1,0:T(8,128)S(1)}, u32[]{:S(2)}, u32[]{:S(2)}) %collective-permute-start.13) | collective-permute-done | bytes 524320 | tf_op jit(solution)/shard_map/ppermute | solution.py:337
  227.5 2.5 collective-permute-start.31
  231.4 3.3 %collective-permute-start.33 = (f32[1,256,128]{2,1,0:T(8,128)S(1)}, f32[1,256,128]{2,1,0:T(8,128)S(1)}, u32[]{:S(2)}, u32[]{:S(2)}) collective-permute-start(f32[1,256,128]{2,1,0:T(8,128)S(1)} %get-tuple-element.33), channel_id=1, source_target_pairs={{0,6},{1,7},{2,4},{3,5},{4,2},{5,3},{6,0},{7,1},{8,14},{9,15},{10,... | collective-permute-start | bytes 393224 | tf_op jit(solution)/shard_map/ppermute | solution.py:370
  240.2 5.8 %inbound.2.rest_8_ = f32[6,256,256]{2,1,0:T(8,128)} custom-call(s32[3,6]{1,0:T(4,128)} %get-tuple-element.40.table, s32[6,1,256]{2,1,0:T(1,128)} %broadcast_in_dim.126.perm, f32[6,256,256]{2,1,0:T(8,128)} %tiles.3, f32[6,256,1]{2,1,0:T(8,128)} %copy.14.energy, f32[8,256,128]{2,1,0:T(8,128)} %all-to-all-done.1.rest_0_), custom_call_target="tpu_custom_call" | custom-call | tf_op jit(solution)/shard_map/inbound/pallas_call | solution.py:135
  246.1 3.4 %collective-permute-done.32.rest_5_ = f32[1,256,128]{2,1,0:T(8,128)S(1)} collective-permute-done((f32[1,256,128]{2,1,0:T(8,128)S(1)}, f32[1,256,128]{2,1,0:T(8,128)S(1)}, u32[]{:S(2)}, u32[]{:S(2)}) %collective-permute-start.32) | collective-permute-done | bytes 131104 | tf_op jit(solution)/shard_map/ppermute | solution.py:370
  250.2 5.8 %inbound.3 = f32[6,256,256]{2,1,0:T(8,128)} custom-call(s32[3,6]{1,0:T(4,128)} %get-tuple-element.41.table, s32[6,1,256]{2,1,0:T(1,128)} %broadcast_in_dim.126.perm, f32[6,256,256]{2,1,0:T(8,128)} %tiles.3, f32[6,256,1]{2,1,0:T(8,128)} %copy.14.energy, f32[1,256,128]{2,1,0:T(8,128)} %get-tuple-element.39.rest_0_, ...), custom_call_target="tpu_custom_call", output_to_operand_aliasing={{}: (12, {})} | custom-call | tf_op jit(solution)/shard_map/inbound/pallas_call | solution.py:135
  (154 shorter events, 75.4 us)
Async XLA Ops:
  6.0 44.4 %all-to-all-start = ((f32[8,6,32,256]{3,2,1,0:T(8,128)}), f32[8,6,32,256]{3,2,1,0:T(8,128)S(1)}, u32[]{:S(2)}, u32[]{:S(2)}) async-start(f32[8,6,32,256]{3,2,1,0:T(8,128)} %bitcast.37), calls=%async_computation | async-start | bytes 3145728 | tf_op jit(solution)/shard_map/all_to_all | solution.py:31
  59.9 15.0 %collective-permute-start.17 = (f32[256,512]{1,0:T(8,128)S(1)}, f32[256,512]{1,0:T(8,128)}, u32[]{:S(2)}, u32[]{:S(2)}) collective-permute-start(f32[256,512]{1,0:T(8,128)S(1)} %pad_maximum_fusion.1.refs_8_), channel_id=1, source_target_pairs={{0,2},{1,3},{2,0},{3,1},{4,6},{5,7},{6,4},{7,5},{8,10},{9,11},{10,... | collective-permute-start | bytes 1572872 | tf_op jit(solution)/shard_map/ppermute | solution.py:47
  68.7 32.9 %collective-permute-start.24 = (f32[256,512]{1,0:T(8,128)S(1)}, f32[256,512]{1,0:T(8,128)S(1)}, u32[]{:S(2)}, u32[]{:S(2)}) collective-permute-start(f32[256,512]{1,0:T(8,128)S(1)} %pad_maximum_fusion.1.refs_8_), channel_id=1, source_target_pairs={{0,1},{1,0},{2,3},{3,2},{4,5},{5,4},{6,7},{7,6},{8,9},{9,8},{10,11... | collective-permute-start | bytes 1572872 | tf_op jit(solution)/shard_map/ppermute | solution.py:302
  70.2 21.5 %collective-permute-start.5 = (f32[256,512]{1,0:T(8,128)S(1)}, f32[256,512]{1,0:T(8,128)}, u32[]{:S(2)}, u32[]{:S(2)}) collective-permute-start(f32[256,512]{1,0:T(8,128)S(1)} %pad_maximum_fusion.refs_6_), channel_id=1, source_target_pairs={{0,2},{1,3},{2,0},{3,1},{4,6},{5,7},{6,4},{7,5},{8,10},{9,11},{10,... | collective-permute-start | bytes 1572872 | tf_op jit(solution)/shard_map/ppermute | solution.py:47
  71.1 31.9 %collective-permute-start.3 = (f32[256,512]{1,0:T(8,128)S(1)}, f32[256,512]{1,0:T(8,128)}, u32[]{:S(2)}, u32[]{:S(2)}) collective-permute-start(f32[256,512]{1,0:T(8,128)S(1)} %pad_maximum_fusion.refs_6_), channel_id=1, source_target_pairs={{2,4},{3,5},{4,2},{5,3},{10,12},{11,13},{12,10},{13,11},{18,20},{1... | collective-permute-start | bytes 1572872 | tf_op jit(solution)/shard_map/ppermute | solution.py:47
  72.6 24.3 %collective-permute-start.22 = (f32[256,512]{1,0:T(8,128)S(1)}, f32[256,512]{1,0:T(8,128)}, u32[]{:S(2)}, u32[]{:S(2)}) collective-permute-start(f32[256,512]{1,0:T(8,128)S(1)} %collective-permute-done.21), channel_id=1, source_target_pairs={{2,0},{3,1},{4,6},{5,7},{10,8},{11,9},{12,14},{13,15},{18,16},{19,... | collective-permute-start | bytes 1572872 | tf_op jit(solution)/shard_map/ppermute | solution.py:47
  74.9 23.5 %collective-permute-start.19 = (f32[256,512]{1,0:T(8,128)}, f32[256,512]{1,0:T(8,128)}, u32[]{:S(2)}, u32[]{:S(2)}) collective-permute-start(f32[256,512]{1,0:T(8,128)} %collective-permute-done.17.refs_9_), channel_id=1, source_target_pairs={{2,4},{3,5},{4,2},{5,3},{10,12},{11,13},{12,10},{13,11},{18,20},{1... | collective-permute-start | bytes 1572872 | tf_op jit(solution)/shard_map/ppermute | solution.py:47
  91.7 58.7 %collective-permute-start.10 = (f32[256,512]{1,0:T(8,128)S(1)}, f32[256,512]{1,0:T(8,128)}, u32[]{:S(2)}, u32[]{:S(2)}) collective-permute-start(f32[256,512]{1,0:T(8,128)S(1)} %pad_maximum_fusion.refs_6_), channel_id=1, source_target_pairs={{0,1},{1,0},{2,3},{3,2},{4,5},{5,4},{6,7},{7,6},{8,9},{9,8},{10,11... | collective-permute-start | bytes 1572872 | tf_op jit(solution)/shard_map/ppermute | solution.py:302
  98.3 17.0 %collective-permute-start.20 = (f32[256,512]{1,0:T(8,128)}, f32[256,512]{1,0:T(8,128)}, u32[]{:S(2)}, u32[]{:S(2)}) collective-permute-start(f32[256,512]{1,0:T(8,128)} %collective-permute-done.19), channel_id=1, source_target_pairs={{2,0},{3,1},{4,6},{5,7},{10,8},{11,9},{12,14},{13,15},{18,16},{19,... | collective-permute-start | bytes 1572872 | tf_op jit(solution)/shard_map/ppermute | solution.py:47
  101.6 36.3 %collective-permute-start.18 = (f32[256,512]{1,0:T(8,128)}, f32[256,512]{1,0:T(8,128)}, u32[]{:S(2)}, u32[]{:S(2)}) collective-permute-start(f32[256,512]{1,0:T(8,128)} %collective-permute-done.17.refs_9_), channel_id=1, source_target_pairs={{0,1},{1,0},{2,3},{3,2},{4,5},{5,4},{6,7},{7,6},{8,9},{9,8},{10,11... | collective-permute-start | bytes 1572872 | tf_op jit(solution)/shard_map/ppermute | solution.py:302
  103.0 23.5 %collective-permute-start.4 = (f32[256,512]{1,0:T(8,128)}, f32[256,512]{1,0:T(8,128)S(1)}, u32[]{:S(2)}, u32[]{:S(2)}) collective-permute-start(f32[256,512]{1,0:T(8,128)} %collective-permute-done.3), channel_id=1, source_target_pairs={{2,0},{3,1},{4,6},{5,7},{10,8},{11,9},{12,14},{13,15},{18,16},{19,... | collective-permute-start | bytes 1572872 | tf_op jit(solution)/shard_map/ppermute | solution.py:47
  111.5 27.1 %collective-permute-start.23 = (f32[256,512]{1,0:T(8,128)S(1)}, f32[256,512]{1,0:T(8,128)S(1)}, u32[]{:S(2)}, u32[]{:S(2)}) collective-permute-start(f32[256,512]{1,0:T(8,128)S(1)} %copy-done.6), channel_id=1, source_target_pairs={{0,1},{1,0},{2,3},{3,2},{4,5},{5,4},{6,7},{7,6},{8,9},{9,8},{10,11... | collective-permute-start | bytes 1572872 | tf_op jit(solution)/shard_map/ppermute | solution.py:302
  115.3 21.0 %collective-permute-start.8 = (f32[256,512]{1,0:T(8,128)}, f32[256,512]{1,0:T(8,128)S(1)}, u32[]{:S(2)}, u32[]{:S(2)}) collective-permute-start(f32[256,512]{1,0:T(8,128)} %collective-permute-done.7), channel_id=1, source_target_pairs={{2,0},{3,1},{4,6},{5,7},{10,8},{11,9},{12,14},{13,15},{18,16},{19,... | collective-permute-start | bytes 1572872 | tf_op jit(solution)/shard_map/ppermute | solution.py:47
  126.5 20.6 %collective-permute-start.25 = (f32[256,512]{1,0:T(8,128)}, f32[256,512]{1,0:T(8,128)}, u32[]{:S(2)}, u32[]{:S(2)}) collective-permute-start(f32[256,512]{1,0:T(8,128)} %broadcast_select_fusion.1.refs_7_), channel_id=1, source_target_pairs={{0,1},{1,0},{2,3},{3,2},{4,5},{5,4},{6,7},{7,6},{8,9},{9,8},{10,11... | collective-permute-start | bytes 1572872 | tf_op jit(solution)/shard_map/ppermute | solution.py:302
  136.4 19.8 %collective-permute-start.6 = (f32[256,512]{1,0:T(8,128)}, f32[256,512]{1,0:T(8,128)}, u32[]{:S(2)}, u32[]{:S(2)}) collective-permute-start(f32[256,512]{1,0:T(8,128)} %collective-permute-done.5.refs_7_), channel_id=1, source_target_pairs={{0,1},{1,0},{2,3},{3,2},{4,5},{5,4},{6,7},{7,6},{8,9},{9,8},{10,11... | collective-permute-start | bytes 1572872 | tf_op jit(solution)/shard_map/ppermute | solution.py:302
  137.9 24.8 %collective-permute-start.9 = (f32[256,512]{1,0:T(8,128)S(1)}, f32[256,512]{1,0:T(8,128)}, u32[]{:S(2)}, u32[]{:S(2)}) collective-permute-start(f32[256,512]{1,0:T(8,128)S(1)} %broadcast_select_fusion.3.refs_8_), channel_id=1, source_target_pairs={{0,1},{1,0},{2,3},{3,2},{4,5},{5,4},{6,7},{7,6},{8,9},{9,8},{10,11... | collective-permute-start | bytes 1572872 | tf_op jit(solution)/shard_map/ppermute | solution.py:302
  139.4 33.2 %collective-permute-start.11 = (f32[256,512]{1,0:T(8,128)S(1)}, f32[256,512]{1,0:T(8,128)S(1)}, u32[]{:S(2)}, u32[]{:S(2)}) collective-permute-start(f32[256,512]{1,0:T(8,128)S(1)} %broadcast_select_fusion.2.refs_10_), channel_id=1, source_target_pairs={{0,1},{1,0},{2,3},{3,2},{4,5},{5,4},{6,7},{7,6},{8,9},{9,8},{10,11... | collective-permute-start | bytes 1572872 | tf_op jit(solution)/shard_map/ppermute | solution.py:302
  150.4 27.6 %collective-permute-start.26 = (f32[1024,256]{1,0:T(8,128)}, f32[1024,256]{1,0:T(8,128)}, u32[]{:S(2)}, u32[]{:S(2)}) collective-permute-start(f32[1024,256]{1,0:T(8,128)} %slice_add_fusion), channel_id=1, source_target_pairs={{0,8},{8,0},{16,24},{24,16},{1,9},{9,1},{17,25},{25,17},{2,10},{10... | collective-permute-start | bytes 3145736 | tf_op jit(solution)/shard_map/ppermute | solution.py:337
  176.0 29.3 %collective-permute-start.12 = (f32[1024,256]{1,0:T(8,128)}, f32[1024,256]{1,0:T(8,128)}, u32[]{:S(2)}, u32[]{:S(2)}) collective-permute-start(f32[1024,256]{1,0:T(8,128)} %slice_add_fusion.2), channel_id=1, source_target_pairs={{0,8},{8,0},{16,24},{24,16},{1,9},{9,1},{17,25},{25,17},{2,10},{10... | collective-permute-start | bytes 3145736 | tf_op jit(solution)/shard_map/ppermute | solution.py:337
  196.2 44.1 %all-to-all-start.1 = ((f32[8,256,128]{2,1,0:T(8,128)}), f32[8,256,128]{2,1,0:T(8,128)}, u32[]{:S(2)}, u32[]{:S(2)}) async-start(f32[8,256,128]{2,1,0:T(8,128)} %gather_fusion.10), calls=%async_computation.1 | async-start | bytes 2097152 | tf_op jit(solution)/shard_map/all_to_all | solution.py:31
  227.3 18.8 %collective-permute-start.30 = (f32[1,256,128]{2,1,0:T(8,128)S(1)}, f32[1,256,128]{2,1,0:T(8,128)S(1)}, u32[]{:S(2)}, u32[]{:S(2)}) collective-permute-start(f32[1,256,128]{2,1,0:T(8,128)S(1)} %get-tuple-element.36), channel_id=1, source_target_pairs={{0,3},{1,2},{2,1},{3,0},{4,7},{5,6},{6,5},{7,4},{8,11},{9,10},{10,... | collective-permute-start | bytes 393224 | tf_op jit(solution)/shard_map/ppermute | solution.py:370
  227.5 18.5 %collective-permute-start.31 = (f32[1,256,128]{2,1,0:T(8,128)S(1)}, f32[1,256,128]{2,1,0:T(8,128)S(1)}, u32[]{:S(2)}, u32[]{:S(2)}) collective-permute-start(f32[1,256,128]{2,1,0:T(8,128)S(1)} %get-tuple-element.35), channel_id=1, source_target_pairs={{0,4},{1,5},{2,6},{3,7},{4,0},{5,1},{6,2},{7,3},{8,12},{9,13},{10,... | collective-permute-start | bytes 393224 | tf_op jit(solution)/shard_map/ppermute | solution.py:370
  230.0 19.5 %collective-permute-start.32 = (f32[1,256,128]{2,1,0:T(8,128)S(1)}, f32[1,256,128]{2,1,0:T(8,128)S(1)}, u32[]{:S(2)}, u32[]{:S(2)}) collective-permute-start(f32[1,256,128]{2,1,0:T(8,128)S(1)} %get-tuple-element.34), channel_id=1, source_target_pairs={{0,5},{1,4},{2,7},{3,6},{4,1},{5,0},{6,3},{7,2},{8,13},{9,12},{10,... | collective-permute-start | bytes 393224 | tf_op jit(solution)/shard_map/ppermute | solution.py:370
  231.4 18.1 %collective-permute-start.33 = (f32[1,256,128]{2,1,0:T(8,128)S(1)}, f32[1,256,128]{2,1,0:T(8,128)S(1)}, u32[]{:S(2)}, u32[]{:S(2)}) collective-permute-start(f32[1,256,128]{2,1,0:T(8,128)S(1)} %get-tuple-element.33), channel_id=1, source_target_pairs={{0,6},{1,7},{2,4},{3,5},{4,2},{5,3},{6,0},{7,1},{8,14},{9,15},{10,... | collective-permute-start | bytes 393224 | tf_op jit(solution)/shard_map/ppermute | solution.py:370
  (35 other events, 295.5 us)
